TPU v7x, 128 devices: a whole 4x4x4 slice. The times are simulated.
128 devices in a mesh: ia: 16 (over y, x), ja: 4 (over z_lo, core), col: 2 (over z_hi).
Axes of the slice: x: 4, y: 4, z: 4 (z_hi: 2, z_lo: 2; z = z_hi * 2 + z_lo), core: 2. Of those that a mesh axis runs over, the one named last changes fastest.
Arguments:
- pair_rep: bfloat16 [512, 512, 128], P('ia', 'ja'), may hold values from -6 to 6
- norm_gain: float32 [128], replicated, may hold values from 0.1 to 1.9
- weights: bfloat16 [4, 128, 128], P(None, None, 'col'), may hold values from -0.5 to 0.5
- residue_mask: int32 [512], replicated, may hold values 0 or 1
- product_grad: bfloat16 [512, 128, 512], P('ia', 'col', 'ja'), may hold values from -1 to 1
Outputs:
- pair_grad: bfloat16 [512, 512, 128], P('ia', 'ja')
- weight_grads: float32 [4, 128, 128], P(None, None, 'col')
All inputs are finite; a program needn't handle non-finite values.
Results may differ from a plain program's by a relative error of at most 0.0067.
Values may be sent and summed in bfloat16 or wider, within the bound.
No kernel may reach another device: no remote copies, remote signals or barrier semaphores. Data moves between devices by JAX's collectives and lax.ppermute only.
A program may use at most 128 MiB of HBM per device.

v0:
```python
import jax
import jax.numpy as jnp
from jax import lax
from jax.experimental import pallas as pl
from jax.experimental.pallas import tpu as pltpu
from jax.sharding import PartitionSpec as P


CLIP_LIMIT = 64.0
BF, F32 = jnp.bfloat16, jnp.float32
NN = (((1,), (0,)), ((), ()))
NT = (((1,), (1,)), ((), ()))
TN = (((0,), (0,)), ((), ()))
KEPT = pl.BlockSpec(memory_space=pltpu.VMEM)
SCALARS = pl.BlockSpec(memory_space=pltpu.SMEM)
MIB = 2**20


def dot(a, b, dims=NN):
    return lax.dot_general(a, b, dims, preferred_element_type=F32)


def kept(x):
    return pltpu.with_memory_space_constraint(x, pltpu.VMEM)


def in_vmem(shape, dtype):
    return pltpu.VMEM(shape, dtype)


def identity(size):
    row = lax.broadcasted_iota(jnp.int32, (size, size), 0)
    col = lax.broadcasted_iota(jnp.int32, (size, size), 1)
    return (row == col).astype(F32)


def local(kernel, out_shape, args, scratch, specs=None, flops=10**6, moved=MIB, limit=24):
    return pl.pallas_call(
        kernel,
        out_shape=out_shape,
        in_specs=specs or [KEPT] * len(args),
        out_specs=jax.tree.map(lambda _: KEPT, out_shape),
        scratch_shapes=scratch,
        compiler_params=pltpu.CompilerParams(vmem_limit_bytes=limit * MIB),
        cost_estimate=pl.CostEstimate(flops=flops, bytes_accessed=moved, transcendentals=0),
    )(*args)


def channels_first_kernel(x_ref, out_ref, flat):
    rows, chans, width = x_ref.shape
    flat[...] = x_ref[...].reshape(rows * chans, width).astype(F32)
    for c in range(chans):
        out_ref[c] = flat[pl.ds(c, rows, stride=chans), :].astype(BF)


def channels_first(x):
    rows, chans, width = x.shape
    out = in_vmem((chans, rows, width), BF)
    scratch = [pltpu.VMEM((rows * chans, width), F32)]
    return local(channels_first_kernel, out, [kept(x)], scratch, limit=8)


def project_kernel(axes, unroll, x_ref, gain_ref, w_ref, mask_ref, cols_ref, sides_ref, factors_ref, normed_ref, unit_ref, inv_ref, flat):
    rows, cols, depth = x_ref.shape
    groups, _, per, _, _ = sides_ref.shape
    half = groups * per
    first_row = lax.axis_index(axes[0]) * rows
    centring = (identity(depth) - 1.0 / depth).astype(BF)
    gain = jnp.concatenate([gain_ref[...]] * 2, axis=1)
    w = w_ref[...]
    valid_cols = cols_ref[pl.ds(lax.axis_index(axes[1]), 1), :].astype(F32)

    def pair(p, carry):
        x = x_ref[pl.ds(2 * p, 2)].reshape(2 * cols, depth)
        centred = dot(centring, x, NT)
        inv_std = lax.rsqrt(jnp.mean(centred * centred, axis=0, keepdims=True) + 1e-05)
        unit = centred * inv_std
        normed = (unit * gain).astype(BF)
        unit_ref[p] = unit
        inv_ref[pl.ds(p, 1), :] = inv_std
        normed_ref[p] = normed
        proj = dot(w, normed)
        valid = jnp.concatenate([valid_cols * mask_ref[first_row + 2 * p + e].astype(F32) for e in range(2)], axis=1)
        for side in range(2):
            at = 2 * side * half
            linear = proj[at : at + half]
            gate = jax.nn.sigmoid(proj[at + half : at + 2 * half])
            first = valid * gate
            both = first * linear
            for e in range(2):
                put = pl.multiple_of((2 * p + e) * 2 * half + side * half, half)
                flat[pl.ds(put, half), :] = both[:, e * cols : (e + 1) * cols]
            factors_ref[p, at : at + half, :] = first
            factors_ref[p, at + half : at + 2 * half, :] = both * (1.0 - gate)
        return carry

    lax.fori_loop(0, rows // 2, pair, 0, unroll=unroll)
    for g in range(groups):
        for side in range(2):
            for c in range(per):
                first = side * half + g * per + c
                sides_ref[g, side, c] = flat[pl.ds(first, rows, stride=2 * half), :].astype(BF)


def project(x, gain, w, mask, groups, axes=("ia", "ja"), unroll=2):
    rows, cols, depth = x.shape
    half = w.shape[0] // 4
    per = half // groups
    out = [
        in_vmem((groups, 2, per, rows, cols), BF),
        in_vmem((rows // 2, 4 * half, 2 * cols), F32),
        in_vmem((rows // 2, depth, 2 * cols), BF),
        in_vmem((rows // 2, depth, 2 * cols), F32),
        in_vmem((rows // 2, 2 * cols), F32),
    ]
    args = [kept(x), kept(gain), kept(w), mask, kept(mask.reshape(-1, cols))]
    return local(
        lambda *refs: project_kernel(axes, unroll, *refs),
        out,
        args,
        [pltpu.VMEM((rows * 2 * half, cols), F32)],
        specs=[KEPT, KEPT, KEPT, SCALARS, KEPT],
        flops=6 * 10**9,
        moved=8 * MIB,
    )


def triangle_kernel(axis, sides_ref, *refs):
    *grads, out_ref = refs
    groups, _, per, rows, cols = sides_ref.shape
    share = groups // len(grads)
    here = lax.axis_index(axis)
    for c in range(per):
        left = sides_ref[:, 0, c].reshape(groups * rows, cols)
        total = None
        for t, grad_ref in enumerate(grads):
            first = (here ^ t) * share
            grad = grad_ref[:, c].reshape(groups * rows, cols)
            right = sides_ref[pl.ds(first, share), 1, c].reshape(share * rows, cols)
            part = dot(grad, right)
            total = part if total is None else total + part
            back = dot(grad, left, TN)
            out_ref[pl.ds(first, share), 1, c] = back.astype(BF).reshape(share, rows, cols)
        out_ref[:, 0, c] = total.astype(BF).reshape(groups, rows, cols)


def triangle(sides, grads, axis="ja"):
    return local(
        lambda *refs: triangle_kernel(axis, *refs),
        in_vmem(sides.shape, BF),
        [kept(sides)] + [kept(g) for g in grads],
        [],
        flops=4 * 10**9,
        moved=5 * MIB,
    )


def gate_kernel(unroll, in_ref, factors_ref, normed_ref, w_ref, out_ref, raw_ref, flat):
    groups, _, per, rows, _ = in_ref.shape
    half = groups * per
    for g in range(groups):
        for side in range(2):
            for c in range(per):
                first = (side * half + g * per + c) * rows
                flat[first : first + rows, :] = in_ref[g, side, c].astype(F32)
    raw_ref[...] = jnp.zeros_like(raw_ref)
    w = w_ref[...]

    def pair(p, carry):
        parts = []
        for side in range(2):
            incoming = jnp.concatenate(
                [flat[pl.ds(side * half * rows + 2 * p + e, half, stride=rows), :] for e in range(2)], axis=1
            )
            at = 2 * side * half
            parts.append((incoming * factors_ref[p, at : at + half, :]).astype(BF))
            parts.append((incoming * factors_ref[p, at + half : at + 2 * half, :]).astype(BF))
        grads = jnp.concatenate(parts, axis=0)
        raw_ref[...] += dot(grads, normed_ref[p], NT)
        out_ref[p] = dot(w, grads).astype(BF)
        return carry

    lax.fori_loop(0, rows // 2, pair, 0, unroll=unroll)


def gate(incoming, factors, normed, w, unroll=2):
    groups, _, per, rows, cols = incoming.shape
    out = [in_vmem(normed.shape, BF), in_vmem((w.shape[1], w.shape[0]), F32)]
    return local(
        lambda *refs: gate_kernel(unroll, *refs),
        out,
        [kept(a) for a in (incoming, factors, normed, w)],
        [pltpu.VMEM((2 * groups * per * rows, cols), F32)],
        flops=6 * 10**9,
        moved=8 * MIB,
    )


def finish_kernel(unit_ref, inv_ref, gain_ref, own_ref, other_ref, out_ref):
    step, cols, _ = out_ref.shape
    turn = identity(cols).astype(BF)
    gain = jnp.concatenate([gain_ref[...]] * 2, axis=1)
    base = pl.program_id(0) * (step // 2)
    for q in range(step // 2):
        p = base + q
        unit = unit_ref[p]
        scaled = (own_ref[p].astype(F32) + other_ref[p].astype(F32)) * gain
        mean = jnp.mean(scaled, axis=0, keepdims=True)
        along = jnp.mean(scaled * unit, axis=0, keepdims=True)
        made = (inv_ref[pl.ds(p, 1), :] * (scaled - mean - unit * along)).astype(BF)
        for e in range(2):
            out_ref[2 * q + e] = dot(turn, made[:, e * cols : (e + 1) * cols], NT).astype(BF)


def finish(unit, inv_std, gain, own, other, step):
    pairs, depth, twice = unit.shape
    shape = (2 * pairs, twice // 2, depth)
    return pl.pallas_call(
        finish_kernel,
        grid=(shape[0] // step,),
        in_specs=[KEPT] * 5,
        out_specs=pl.BlockSpec((step,) + shape[1:], lambda r: (r, 0, 0)),
        out_shape=jax.ShapeDtypeStruct(shape, BF),
        compiler_params=pltpu.CompilerParams(vmem_limit_bytes=16 * MIB),
        cost_estimate=pl.CostEstimate(flops=10**9, bytes_accessed=4 * MIB, transcendentals=0),
        name="finish",
    )(*[kept(a) for a in (unit, inv_std, gain, own, other)])


def swapped(x, axis, bit):
    size = lax.axis_size(axis)
    return lax.ppermute(x, axis, [(i, i ^ bit) for i in range(size)])


def on_device(pair_rep, norm_gain, weights, residue_mask, product_grad):
    rows, cols, depth = pair_rep.shape
    chans = product_grad.shape[1]
    groups = lax.axis_size("ia")
    per = chans // groups
    w = jnp.swapaxes(weights, 1, 2).reshape(4 * chans, depth)
    w_back = jnp.swapaxes(w, 0, 1)
    gain = jnp.broadcast_to(norm_gain[:, None], (depth, cols))

    grads = channels_first(product_grad).reshape(groups, per, rows, cols)
    grads = lax.all_to_all(grads, "ia", 0, 0, tiled=True)
    sides, factors, normed, unit, inv_std = project(pair_rep, gain, w, residue_mask, groups)
    grads, sides = lax.optimization_barrier((grads, sides))
    far = swapped(grads, "ja", 2)
    sides = lax.all_to_all(sides, "ia", 0, 0, tiled=True)
    near = swapped(grads, "ja", 1)
    farther = swapped(far, "ja", 1)
    products = triangle(sides, (grads, near, far, farther))
    products = lax.all_to_all(products, "ia", 0, 0, tiled=True)
    own, raw = gate(products, factors, normed, w_back)
    raw = raw + swapped(raw, "ja", 2)
    other = swapped(own, "col", 1)
    raw = raw + swapped(raw, "ja", 1)
    pieces = lax.all_to_all(raw.reshape(groups, -1, depth), "ia", 0, 0, tiled=True)
    piece = jnp.sum(pieces, axis=0)
    whole = lax.all_to_all(jnp.broadcast_to(piece[None], pieces.shape), "ia", 0, 0, tiled=True)
    whole = whole.reshape(4, chans, depth)
    squares = jnp.sum(whole * whole).reshape(1, 1)
    others = swapped(squares, "col", 1)
    pair_grad = finish(unit, inv_std, gain, own, other, 8)
    others, pair_grad = lax.optimization_barrier((others, pair_grad))
    factor = jnp.minimum(1.0, CLIP_LIMIT * lax.rsqrt((squares + others)[0, 0] + 1e-06))
    weight_grads = jnp.swapaxes(whole, 1, 2) * factor
    return (pair_grad, weight_grads)


def solution(mesh):
    placed = (P("ia", "ja", None), P(), P(None, None, "col"), P(), P("ia", "col", "ja"))
    return jax.shard_map(
        on_device,
        mesh=mesh,
        in_specs=placed,
        out_specs=(P("ia", "ja", None), P(None, None, "col")),
        check_vma=False,
    )
```

profile of v0, /device:TPU:0, one launch (start us, length us, event | category | flops | bytes accessed | tf_op | source)
XLA Modules:
  0.0 141.3 jit_solution(8184657515625696807)
XLA Ops:
  0.6 1.0 copy-done.1
  1.7 1.5 %shard_map.68 = bf16[64,32,128]{2,1,0:T(8,128)(2,1)} custom-call(bf16[32,64,128]{2,1,0:T(8,128)(2,1)S(1)} %copy-done.1), custom_call_target="tpu_custom_call" | custom-call | flops 1000000 | bytes 1048576 | tf_op jit(solution)/shard_map/pallas_call | solution.py:38
  3.1 7.2 %all-to-all-start = ((bf16[16,4,32,128]{3,2,1,0:T(8,128)(2,1)}), bf16[16,4,32,128]{3,2,1,0:T(8,128)(2,1)}, u32[]{:S(2)}, u32[]{:S(2)}) async-start(bf16[16,4,32,128]{3,2,1,0:T(8,128)(2,1)} %bitcast), calls=%async_computation | async-start | bytes 1048576 | tf_op jit(solution)/shard_map/all_to_all | solution.py:245
  11.9 1.2 copy-done.4
  13.8 6.5 %shard_map.69 = (bf16[16,2,4,32,128]{4,3,2,1,0:T(8,128)(2,1)}, f32[16,256,256]{2,1,0:T(8,128)S(1)}, bf16[16,128,256]{2,1,0:T(8,128)(2,1)S(1)}, f32[16,128,256]{2,1,0:T(8,128)S(1)}, f32[16,256]{1,0:T(8,128)S(1)}) custom-call(bf16[32,128,128]{2,1,0:T(8,128)(2,1)S(1)} %copy-done.4, f32[128,128]{1,0:T(8,128)S(1)} %broadcast_in_dim.4.refs_1_.gain_ref, ...), custom_call_target="tpu_custom_call" | custom-call | flops 6000000000 | bytes 8388608 | tf_op jit(solution)/shard_map/pallas_call | solution.py:38
  20.3 1.9 %copy-done.8 = f32[16,256,256]{2,1,0:T(8,128)} copy-done((f32[16,256,256]{2,1,0:T(8,128)}, f32[16,256,256]{2,1,0:T(8,128)S(1)}, u32[]{:S(2)}) %copy-start.8) | copy-done | bytes 4194328
  22.2 1.0 copy-done.10
  23.2 1.9 %collective-permute-start.1 = (bf16[16,4,32,128]{3,2,1,0:T(8,128)(2,1)}, bf16[16,4,32,128]{3,2,1,0:T(8,128)(2,1)}, u32[]{:S(2)}, u32[]{:S(2)}) collective-permute-start(bf16[16,4,32,128]{3,2,1,0:T(8,128)(2,1)} %all-to-all-done.refs_1_), channel_id=1, source_target_pairs={{0,4},{2,6},{4,0},{6,2},{1,5},{3,7},{5,1},{7,3},{8,12},{10,14},{12... | collective-permute-start | bytes 1572872 | tf_op jit(solution)/shard_map/ppermute | solution.py:232
  25.1 7.2 %all-to-all-start.1 = ((bf16[16,2,4,32,128]{4,3,2,1,0:T(8,128)(2,1)}), bf16[16,2,4,32,128]{4,3,2,1,0:T(8,128)(2,1)S(1)}, u32[]{:S(2)}, u32[]{:S(2)}) async-start(bf16[16,2,4,32,128]{4,3,2,1,0:T(8,128)(2,1)} %get-tuple-element.14), calls=%async_computation.1 | async-start | bytes 2097152 | tf_op jit(solution)/shard_map/all_to_all | solution.py:249
  32.4 4.7 %collective-permute-done.1.refs_3_ = bf16[16,4,32,128]{3,2,1,0:T(8,128)(2,1)} collective-permute-done((bf16[16,4,32,128]{3,2,1,0:T(8,128)(2,1)}, bf16[16,4,32,128]{3,2,1,0:T(8,128)(2,1)}, u32[]{:S(2)}, u32[]{:S(2)}) %collective-permute-start.1) | collective-permute-done | bytes 524320 | tf_op jit(solution)/shard_map/ppermute | solution.py:232
  37.9 11.0 %all-to-all-done.1.refs_0_ = bf16[16,2,4,32,128]{4,3,2,1,0:T(8,128)(2,1)S(1)} async-done(((bf16[16,2,4,32,128]{4,3,2,1,0:T(8,128)(2,1)}), bf16[16,2,4,32,128]{4,3,2,1,0:T(8,128)(2,1)S(1)}, u32[]{:S(2)}, u32[]{:S(2)}) %all-to-all-start.1) | async-done | bytes 1048608 | tf_op jit(solution)/shard_map/all_to_all | solution.py:249
  48.8 1.0 copy-done.6
  49.9 2.6 %shard_map.70 = bf16[16,2,4,32,128]{4,3,2,1,0:T(8,128)(2,1)S(1)} custom-call(bf16[16,2,4,32,128]{4,3,2,1,0:T(8,128)(2,1)S(1)} %all-to-all-done.1.refs_0_, bf16[16,4,32,128]{3,2,1,0:T(8,128)(2,1)} %all-to-all-done.refs_1_, bf16[16,4,32,128]{3,2,1,0:T(8,128)(2,1)S(1)} %copy-done.6, bf16[16,4,32,128]{3,2,1,0:T(8,128)(2,1)} %collective-permute-done.1.refs_3_, ...), custom_call_target="tpu_custom_call" | custom-call | flops 4000000000 | bytes 5242880 | tf_op jit(solution)/shard_map/pallas_call | solution.py:38
  53.5 3.7 %all-to-all-start.2 = ((bf16[16,2,4,32,128]{4,3,2,1,0:T(8,128)(2,1)}), bf16[16,2,4,32,128]{4,3,2,1,0:T(8,128)(2,1)S(1)}, u32[]{:S(2)}, u32[]{:S(2)}) async-start(bf16[16,2,4,32,128]{4,3,2,1,0:T(8,128)(2,1)} %copy-done), calls=%async_computation.2 | async-start | bytes 2097152 | tf_op jit(solution)/shard_map/all_to_all | solution.py:253
  57.3 16.4 %all-to-all-done.2.refs_0_ = bf16[16,2,4,32,128]{4,3,2,1,0:T(8,128)(2,1)S(1)} async-done(((bf16[16,2,4,32,128]{4,3,2,1,0:T(8,128)(2,1)}), bf16[16,2,4,32,128]{4,3,2,1,0:T(8,128)(2,1)S(1)}, u32[]{:S(2)}, u32[]{:S(2)}) %all-to-all-start.2) | async-done | bytes 1048608 | tf_op jit(solution)/shard_map/all_to_all | solution.py:253
  73.7 2.2 %copy-done.9 = f32[16,256,256]{2,1,0:T(8,128)S(1)} copy-done((f32[16,256,256]{2,1,0:T(8,128)S(1)}, f32[16,256,256]{2,1,0:T(8,128)}, u32[]{:S(2)}) %copy-start.9) | copy-done | bytes 4194328
  75.9 1.2 copy-done.11
  77.1 3.9 %shard_map.71 = (bf16[16,128,256]{2,1,0:T(8,128)(2,1)}, f32[256,128]{1,0:T(8,128)S(1)}) custom-call(bf16[16,2,4,32,128]{4,3,2,1,0:T(8,128)(2,1)S(1)} %all-to-all-done.2.refs_0_, f32[16,256,256]{2,1,0:T(8,128)S(1)} %copy-done.9, bf16[16,128,256]{2,1,0:T(8,128)(2,1)S(1)} %copy-done.11, bf16[128,256]{1,0:T(8,128)(2,1)S(1)} %bitcast.14), custom_call_target="tpu_custom_call" | custom-call | flops 6000000000 | bytes 8388608 | tf_op jit(solution)/shard_map/pallas_call | solution.py:38
  81.1 3.6 %collective-permute-start.6 = (bf16[16,128,256]{2,1,0:T(8,128)(2,1)}, bf16[16,128,256]{2,1,0:T(8,128)(2,1)S(1)}, u32[]{:S(2)}, u32[]{:S(2)}) collective-permute-start(bf16[16,128,256]{2,1,0:T(8,128)(2,1)} %get-tuple-element.21.own_ref), channel_id=1, source_target_pairs={{0,1},{1,0},{2,3},{3,2},{4,5},{5,4},{6,7},{7,6},{8,9},{9,8},{10,11... | collective-permute-start | bytes 3145736 | tf_op jit(solution)/shard_map/ppermute | solution.py:232
  84.6 23.3 %collective-permute-done.3 = f32[256,128]{1,0:T(8,128)S(1)} collective-permute-done((f32[256,128]{1,0:T(8,128)S(1)}, f32[256,128]{1,0:T(8,128)S(1)}, u32[]{:S(2)}, u32[]{:S(2)}) %collective-permute-start.3) | collective-permute-done | bytes 131104 | tf_op jit(solution)/shard_map/ppermute | solution.py:232
  108.0 1.3 collective-permute-done.4
  109.4 13.0 %all_to_all.25 = f32[16,16,128]{2,1,0:T(8,128)S(1)} all-to-all(f32[16,16,128]{2,1,0:T(8,128)S(1)} %bitcast.16), channel_id=1, replica_groups=mesh['ia'=16,'ja'=4,'col'=2] {'ia'}, dimensions={0} | all-to-all | bytes 262144 | tf_op jit(solution)/shard_map/all_to_all | solution.py:258
  122.4 11.1 %all_to_all.26 = f32[16,16,128]{2,1,0:T(8,128)S(1)} all-to-all(f32[16,16,128]{2,1,0:T(8,128)S(1)} %broadcast_in_dim.5), channel_id=1, replica_groups=mesh['ia'=16,'ja'=4,'col'=2] {'ia'}, dimensions={0} | all-to-all | bytes 262144 | tf_op jit(solution)/shard_map/all_to_all | solution.py:260
  135.0 3.9 %finish.1 = bf16[32,128,128]{2,1,0:T(8,128)(2,1)} custom-call(f32[16,128,256]{2,1,0:T(8,128)S(1)} %get-tuple-element.19.unit_ref, f32[16,256]{1,0:T(8,128)S(1)} %get-tuple-element.20.inv_ref, f32[128,128]{1,0:T(8,128)S(1)} %broadcast_in_dim.4.refs_1_.gain_ref, bf16[16,128,256]{2,1,0:T(8,128)(2,1)} %get-tuple-element.21.own_ref, ...), custom_call_target="tpu_custom_call" | custom-call | flops 1000000000 | bytes 4194304 | tf_op jit(solution)/shard_map/finish/pallas_call | solution.py:218
  (35 shorter events, 7.1 us)
Async XLA Ops:
  0.6 1.0 copy-start.1
  3.1 20.1 %all-to-all-start = ((bf16[16,4,32,128]{3,2,1,0:T(8,128)(2,1)}), bf16[16,4,32,128]{3,2,1,0:T(8,128)(2,1)}, u32[]{:S(2)}, u32[]{:S(2)}) async-start(bf16[16,4,32,128]{3,2,1,0:T(8,128)(2,1)} %bitcast), calls=%async_computation | async-start | bytes 1048576 | tf_op jit(solution)/shard_map/all_to_all | solution.py:245
  11.1 0.9 copy-start.2
  11.9 1.2 copy-start.4
  13.1 0.7 copy-start.7
  20.3 1.9 %copy-start.8 = (f32[16,256,256]{2,1,0:T(8,128)}, f32[16,256,256]{2,1,0:T(8,128)S(1)}, u32[]{:S(2)}) copy-start(f32[16,256,256]{2,1,0:T(8,128)S(1)} %get-tuple-element.16.refs_1_) | copy-start | bytes 12582916
  22.2 1.0 copy-start.10
  23.2 13.9 %collective-permute-start.1 = (bf16[16,4,32,128]{3,2,1,0:T(8,128)(2,1)}, bf16[16,4,32,128]{3,2,1,0:T(8,128)(2,1)}, u32[]{:S(2)}, u32[]{:S(2)}) collective-permute-start(bf16[16,4,32,128]{3,2,1,0:T(8,128)(2,1)} %all-to-all-done.refs_1_), channel_id=1, source_target_pairs={{0,4},{2,6},{4,0},{6,2},{1,5},{3,7},{5,1},{7,3},{8,12},{10,14},{12... | collective-permute-start | bytes 1572872 | tf_op jit(solution)/shard_map/ppermute | solution.py:232
  25.1 23.7 %all-to-all-start.1 = ((bf16[16,2,4,32,128]{4,3,2,1,0:T(8,128)(2,1)}), bf16[16,2,4,32,128]{4,3,2,1,0:T(8,128)(2,1)S(1)}, u32[]{:S(2)}, u32[]{:S(2)}) async-start(bf16[16,2,4,32,128]{4,3,2,1,0:T(8,128)(2,1)} %get-tuple-element.14), calls=%async_computation.1 | async-start | bytes 2097152 | tf_op jit(solution)/shard_map/all_to_all | solution.py:249
  32.3 24.9 %copy-start.3 = (bf16[4,128,64]{1,2,0:T(8,128)(2,1)S(1)}, bf16[4,128,64]{1,2,0:T(8,128)(2,1)}, u32[]{:S(2)}) copy-start(bf16[4,128,64]{1,2,0:T(8,128)(2,1)} %param.7) | copy-start | bytes 196612
  32.3 4.8 %collective-permute-start = (bf16[16,4,32,128]{3,2,1,0:T(8,128)(2,1)}, bf16[16,4,32,128]{3,2,1,0:T(8,128)(2,1)S(1)}, u32[]{:S(2)}, u32[]{:S(2)}) collective-permute-start(bf16[16,4,32,128]{3,2,1,0:T(8,128)(2,1)} %all-to-all-done.refs_1_), channel_id=1, source_target_pairs={{0,2},{2,0},{4,6},{6,4},{1,3},{3,1},{5,7},{7,5},{8,10},{10,8},{12,... | collective-permute-start | bytes 1572872 | tf_op jit(solution)/shard_map/ppermute | solution.py:232
  37.1 11.8 %collective-permute-start.2 = (bf16[16,4,32,128]{3,2,1,0:T(8,128)(2,1)}, bf16[16,4,32,128]{3,2,1,0:T(8,128)(2,1)}, u32[]{:S(2)}, u32[]{:S(2)}) collective-permute-start(bf16[16,4,32,128]{3,2,1,0:T(8,128)(2,1)} %collective-permute-done.1.refs_3_), channel_id=1, source_target_pairs={{0,2},{2,0},{4,6},{6,4},{1,3},{3,1},{5,7},{7,5},{8,10},{10,8},{12,... | collective-permute-start | bytes 1572872 | tf_op jit(solution)/shard_map/ppermute | solution.py:232
  37.1 0.8 copy-start.5
  48.8 1.0 copy-start.6
  52.5 1.0 copy-start
  53.5 20.2 %all-to-all-start.2 = ((bf16[16,2,4,32,128]{4,3,2,1,0:T(8,128)(2,1)}), bf16[16,2,4,32,128]{4,3,2,1,0:T(8,128)(2,1)S(1)}, u32[]{:S(2)}, u32[]{:S(2)}) async-start(bf16[16,2,4,32,128]{4,3,2,1,0:T(8,128)(2,1)} %copy-done), calls=%async_computation.2 | async-start | bytes 2097152 | tf_op jit(solution)/shard_map/all_to_all | solution.py:253
  73.7 2.2 %copy-start.9 = (f32[16,256,256]{2,1,0:T(8,128)S(1)}, f32[16,256,256]{2,1,0:T(8,128)}, u32[]{:S(2)}) copy-start(f32[16,256,256]{2,1,0:T(8,128)} %copy-done.8) | copy-start | bytes 12582916
  75.9 1.2 copy-start.11
  81.1 53.9 %collective-permute-start.6 = (bf16[16,128,256]{2,1,0:T(8,128)(2,1)}, bf16[16,128,256]{2,1,0:T(8,128)(2,1)S(1)}, u32[]{:S(2)}, u32[]{:S(2)}) collective-permute-start(bf16[16,128,256]{2,1,0:T(8,128)(2,1)} %get-tuple-element.21.own_ref), channel_id=1, source_target_pairs={{0,1},{1,0},{2,3},{3,2},{4,5},{5,4},{6,7},{7,6},{8,9},{9,8},{10,11... | collective-permute-start | bytes 3145736 | tf_op jit(solution)/shard_map/ppermute | solution.py:232
  84.6 23.3 %collective-permute-start.3 = (f32[256,128]{1,0:T(8,128)S(1)}, f32[256,128]{1,0:T(8,128)S(1)}, u32[]{:S(2)}, u32[]{:S(2)}) collective-permute-start(f32[256,128]{1,0:T(8,128)S(1)} %get-tuple-element.18), channel_id=1, source_target_pairs={{0,4},{2,6},{4,0},{6,2},{1,5},{3,7},{5,1},{7,3},{8,12},{10,14},{12... | collective-permute-start | bytes 393224 | tf_op jit(solution)/shard_map/ppermute | solution.py:232
  107.9 1.4 %collective-permute-start.4 = (f32[256,128]{1,0:T(8,128)S(1)}, f32[256,128]{1,0:T(8,128)S(1)}, u32[]{:S(2)}, u32[]{:S(2)}) collective-permute-start(f32[256,128]{1,0:T(8,128)S(1)} %add.13), channel_id=1, source_target_pairs={{0,2},{2,0},{4,6},{6,4},{1,3},{3,1},{5,7},{7,5},{8,10},{10,8},{12,... | collective-permute-start | bytes 393224 | tf_op jit(solution)/shard_map/ppermute | solution.py:232
  134.1 5.3 %collective-permute-start.5 = (f32[1,1]{1,0:T(1,128)}, f32[1,1]{1,0:T(1,128)}, u32[]{:S(2)}, u32[]{:S(2)}) collective-permute-start(f32[1,1]{1,0:T(1,128)} %bitcast.7), channel_id=1, source_target_pairs={{0,1},{1,0},{2,3},{3,2},{4,5},{5,4},{6,7},{7,6},{8,9},{9,8},{10,11... | collective-permute-start | bytes 20 | tf_op jit(solution)/shard_map/ppermute | solution.py:232
where the time goes:
time: 142 us; the launch traced here: 141 us
  waiting for transfers between devices  57.2 us (40%)
  starting transfers between devices  24.6 us (17%)
  blocking collectives  24.1 us (17%)
  Pallas kernels  18.4 us (13%)
  local copies, waits for them, and re-layouts  13.8 us (10%)
  between operations  2 us (1%)
    ppermute x7, waiting for transfers between devices, swapped(): return lax.ppermute(x, axis, [(i, i ^ bit) for i in range(size)])  29.8 us
    all_to_all x1, waiting for transfers between devices, on_device(): products = lax.all_to_all(products, 'ia', 0, 0, tiled=True)  16.4 us
    pallas_call x4, Pallas kernels, local(): pl.pallas_call(kernel, out_shape=out_shape, in_specs=specs or [KEPT] * le...  14.5 us
    all_to_all x1, blocking collectives, on_device(): lax.all_to_all(raw.reshape(groups, -1, depth), 'ia', 0, 0, tiled=True)  13 us
    unnamed x24, local copies, waits for them, and re-layouts  12.9 us
    all_to_all x1, blocking collectives, on_device(): lax.all_to_all(jnp.broadcast_to(piece[None], pieces.shape), 'ia', 0, 0, t...  11.1 us
    all_to_all x1, waiting for transfers between devices, on_device(): sides = lax.all_to_all(sides, 'ia', 0, 0, tiled=True)  11 us
    all_to_all x1, starting transfers between devices, on_device(): grads = lax.all_to_all(grads, 'ia', 0, 0, tiled=True)  7.2 us
  transfers between devices with their start and end apart: 10, of which 6 were waited for; matrix products, arithmetic and copies ran while one was open for 1% of the time, Pallas kernels for 7%

commit v1 on v0

v1 whole, which is shorter than its diff:
```python
import jax
import jax.numpy as jnp
from jax import lax
from jax.experimental import pallas as pl
from jax.experimental.pallas import tpu as pltpu
from jax.sharding import PartitionSpec as P


CLIP_LIMIT = 64.0
BF, F32 = jnp.bfloat16, jnp.float32
NN = (((1,), (0,)), ((), ()))
NT = (((1,), (1,)), ((), ()))
TN = (((0,), (0,)), ((), ()))
KEPT = pl.BlockSpec(memory_space=pltpu.VMEM)
SCALARS = pl.BlockSpec(memory_space=pltpu.SMEM)
MIB = 2**20


def dot(a, b, dims=NN):
    return lax.dot_general(a, b, dims, preferred_element_type=F32)


def kept(x):
    return pltpu.with_memory_space_constraint(x, pltpu.VMEM)


def in_hbm(x):
    return pltpu.with_memory_space_constraint(x, pltpu.HBM)


def identity(size):
    row = lax.broadcasted_iota(jnp.int32, (size, size), 0)
    col = lax.broadcasted_iota(jnp.int32, (size, size), 1)
    return (row == col).astype(F32)


def call(kernel, out_shape, args, in_specs, out_specs, scratch=(), grid=(), flops=10**6, moved=MIB):
    return pl.pallas_call(
        kernel,
        grid=grid,
        out_shape=out_shape,
        in_specs=in_specs,
        out_specs=out_specs,
        scratch_shapes=list(scratch),
        compiler_params=pltpu.CompilerParams(vmem_limit_bytes=24 * MIB),
        cost_estimate=pl.CostEstimate(flops=flops, bytes_accessed=moved, transcendentals=0),
    )(*args)


def fixed(shape):
    return pl.BlockSpec(shape, lambda r: (0,) * len(shape))


def leading(step, shape):
    return pl.BlockSpec((step,) + tuple(shape[1:]), lambda r: (r,) + (0,) * (len(shape) - 1))


def channels_first_kernel(x_ref, out_ref, flat):
    rows, chans, width = x_ref.shape
    flat[...] = x_ref[...].reshape(rows * chans, width).astype(F32)
    for c in range(chans):
        out_ref[c] = flat[pl.ds(c, rows, stride=chans), :].astype(BF)


def channels_first(x, step=16):
    rows, chans, width = x.shape
    return call(
        channels_first_kernel,
        jax.ShapeDtypeStruct((chans, rows, width), BF),
        [x],
        [leading(step, x.shape)],
        pl.BlockSpec((chans, step, width), lambda r: (0, r, 0)),
        [pltpu.VMEM((step * chans, width), F32)],
        (rows // step,),
    )


def project_kernel(axes, unroll, x_ref, gain_ref, w_ref, mask_ref, cols_ref, sides_ref, factors_ref, normed_ref, unit_ref, inv_ref, flat, gains):
    rows, cols, depth = x_ref.shape
    groups, _, per, _, _ = sides_ref.shape
    half = groups * per
    step = pl.program_id(0)
    first_row = lax.axis_index(axes[0]) * (rows * pl.num_programs(0)) + step * rows
    centring = (identity(depth) - 1.0 / depth).astype(BF)

    @pl.when(step == 0)
    def _():
        gains[...] = jnp.broadcast_to(gain_ref[...], (2 * cols, depth)).T

    w = w_ref[...]
    valid_cols = cols_ref[pl.ds(lax.axis_index(axes[1]), 1), :].astype(F32)

    def pair(p, carry):
        x = x_ref[pl.ds(2 * p, 2)].reshape(2 * cols, depth)
        centred = dot(centring, x, NT)
        inv_std = lax.rsqrt(jnp.mean(centred * centred, axis=0, keepdims=True) + 1e-05)
        unit = centred * inv_std
        normed = (unit * gains[...]).astype(BF)
        unit_ref[p] = unit
        inv_ref[p] = inv_std
        whole = step * (rows // 2) + p
        normed_ref[whole] = normed
        proj = dot(w, normed)
        valid = jnp.concatenate([valid_cols * mask_ref[first_row + 2 * p + e].astype(F32) for e in range(2)], axis=1)
        for side in range(2):
            at = 2 * side * half
            linear = proj[at : at + half]
            gate = jax.nn.sigmoid(proj[at + half : at + 2 * half])
            first = valid * gate
            both = first * linear
            for e in range(2):
                put = pl.multiple_of((2 * p + e) * 2 * half + side * half, half)
                flat[pl.ds(put, half), :] = both[:, e * cols : (e + 1) * cols]
            factors_ref[whole, at : at + half, :] = first.astype(BF)
            factors_ref[whole, at + half : at + 2 * half, :] = (both * (1.0 - gate)).astype(BF)
        return carry

    lax.fori_loop(0, rows // 2, pair, 0, unroll=unroll)
    for g in range(groups):
        for side in range(2):
            for c in range(per):
                first = side * half + g * per + c
                sides_ref[g, side, c] = flat[pl.ds(first, rows, stride=2 * half), :].astype(BF)


def project(x, gain, w, mask, groups, axes=("ia", "ja"), unroll=8, step=16):
    rows, cols, depth = x.shape
    half = w.shape[0] // 4
    per = half // groups
    pairs = rows // 2
    out = [
        pltpu.HBM((groups, 2, per, rows, cols), BF),
        pltpu.VMEM((pairs, 4 * half, 2 * cols), BF),
        pltpu.VMEM((pairs, depth, 2 * cols), BF),
        pltpu.HBM((pairs, depth, 2 * cols), F32),
        pltpu.HBM((pairs, 1, 2 * cols), F32),
    ]
    table = mask.reshape(-1, cols)
    return call(
        lambda *refs: project_kernel(axes, unroll, *refs),
        out,
        [in_hbm(x), in_hbm(gain[None]), in_hbm(w), mask, in_hbm(table)],
        [leading(step, x.shape), fixed((1, depth)), fixed(w.shape), SCALARS, fixed(table.shape)],
        [pl.BlockSpec((groups, 2, per, step, cols), lambda r: (0, 0, 0, r, 0))] + [KEPT, KEPT] + [leading(step // 2, o.shape) for o in out[3:]],
        [pltpu.VMEM((step * 2 * half, cols), F32), pltpu.VMEM((depth, 2 * cols), F32)],
        (rows // step,),
        flops=6 * 10**9,
        moved=8 * MIB,
    )


def triangle_kernel(axis, sides_ref, *refs):
    *grads, out_ref = refs
    groups, _, per, rows, cols = sides_ref.shape
    share = groups // len(grads)
    here = lax.axis_index(axis)
    for c in range(per):
        left = sides_ref[:, 0, c].reshape(groups * rows, cols)
        total = None
        for t, grad_ref in enumerate(grads):
            first = (here ^ t) * share
            grad = grad_ref[:, c].reshape(groups * rows, cols)
            right = sides_ref[pl.ds(first, share), 1, c].reshape(share * rows, cols)
            part = dot(grad, right)
            total = part if total is None else total + part
            back = dot(grad, left, TN)
            out_ref[pl.ds(first, share), 1, c] = back.astype(BF).reshape(share, rows, cols)
        out_ref[:, 0, c] = total.astype(BF).reshape(groups, rows, cols)


def triangle(sides, grads, axis="ja"):
    return call(
        lambda *refs: triangle_kernel(axis, *refs),
        pltpu.HBM(sides.shape, BF),
        [kept(sides)] + [in_hbm(g) for g in grads],
        [KEPT] * (1 + len(grads)),
        KEPT,
        flops=4 * 10**9,
        moved=5 * MIB,
    )


def gate_kernel(unroll, in_ref, factors_ref, normed_ref, w_ref, out_ref, raw_ref, flat):
    groups, _, per, rows, _ = in_ref.shape
    half = groups * per
    pairs = out_ref.shape[0]
    step = pl.program_id(0)

    @pl.when(step == 0)
    def _():
        for g in range(groups):
            for side in range(2):
                for c in range(per):
                    first = (side * half + g * per + c) * rows
                    flat[first : first + rows, :] = in_ref[g, side, c].astype(F32)
        raw_ref[...] = jnp.zeros_like(raw_ref)

    w = w_ref[...].T

    def pair(q, carry):
        p = step * pairs + q
        parts = []
        for side in range(2):
            incoming = jnp.concatenate(
                [flat[pl.ds(side * half * rows + 2 * p + e, half, stride=rows), :] for e in range(2)], axis=1
            )
            at = 2 * side * half
            for first in (at, at + half):
                parts.append((incoming * factors_ref[p, first : first + half, :].astype(F32)).astype(BF))
        grads = jnp.concatenate(parts, axis=0)
        raw_ref[...] += dot(grads, normed_ref[p], NT)
        out_ref[q] = dot(w, grads).astype(BF)
        return carry

    lax.fori_loop(0, pairs, pair, 0, unroll=unroll)


def gate(incoming, factors, normed, w, unroll=8, step=8):
    groups, _, per, rows, cols = incoming.shape
    return call(
        lambda *refs: gate_kernel(unroll, *refs),
        [pltpu.HBM(normed.shape, BF), jax.ShapeDtypeStruct(w.shape, F32)],
        [kept(incoming), kept(factors), kept(normed), in_hbm(w)],
        [KEPT, KEPT, KEPT, fixed(w.shape)],
        [leading(step, normed.shape), fixed(w.shape)],
        [pltpu.VMEM((2 * groups * per * rows, cols), F32)],
        (normed.shape[0] // step,),
        flops=6 * 10**9,
        moved=8 * MIB,
    )


def finish_kernel(unit_ref, inv_ref, gain_ref, own_ref, other_ref, out_ref, gains):
    step, cols, depth = out_ref.shape

    @pl.when(pl.program_id(0) == 0)
    def _():
        gains[...] = jnp.broadcast_to(gain_ref[...], (2 * cols, depth)).T

    turn = identity(2 * cols).astype(BF)
    base = pl.program_id(0) * (step // 2)
    for q in range(step // 2):
        unit = unit_ref[q]
        scaled = (own_ref[q].astype(F32) + other_ref[base + q].astype(F32)) * gains[...]
        mean = jnp.mean(scaled, axis=0, keepdims=True)
        along = jnp.mean(scaled * unit, axis=0, keepdims=True)
        made = (inv_ref[q] * (scaled - mean - unit * along)).astype(BF)
        out_ref[pl.ds(2 * q, 2)] = dot(turn, made, NT).astype(BF).reshape(2, cols, depth)


def finish(unit, inv_std, gain, own, other, step=16):
    pairs, depth, twice = unit.shape
    shape = (2 * pairs, twice // 2, depth)
    half = step // 2
    return call(
        finish_kernel,
        jax.ShapeDtypeStruct(shape, BF),
        [in_hbm(unit), in_hbm(inv_std), in_hbm(gain[None]), in_hbm(own), kept(other)],
        [leading(half, unit.shape), leading(half, inv_std.shape), fixed((1, depth)), leading(half, own.shape), KEPT],
        leading(step, shape),
        [pltpu.VMEM((depth, twice), F32)],
        (shape[0] // step,),
        flops=10**9,
        moved=4 * MIB,
    )


def scale_kernel(whole_ref, mine_ref, others_ref, out_ref):
    factor = jnp.minimum(1.0, CLIP_LIMIT * lax.rsqrt(mine_ref[...] + others_ref[...] + 1e-06))
    out_ref[...] = whole_ref[...] * factor


def scale(whole, mine, others):
    return call(scale_kernel, pltpu.HBM(whole.shape, F32), [kept(whole), mine, others], [KEPT] * 3, KEPT)


def swapped(x, axis, bit):
    size = lax.axis_size(axis)
    return lax.ppermute(x, axis, [(i, i ^ bit) for i in range(size)])


def on_device(pair_rep, norm_gain, weights, residue_mask, product_grad):
    rows, cols, depth = pair_rep.shape
    chans = product_grad.shape[1]
    groups = lax.axis_size("ia")
    per = chans // groups
    w = jnp.swapaxes(weights, 1, 2).reshape(4 * chans, depth)

    grads = channels_first(product_grad).reshape(groups, per, rows, cols)
    grads = lax.all_to_all(grads, "ia", 0, 0, tiled=True)
    sides, factors, normed, unit, inv_std = project(pair_rep, norm_gain, w, residue_mask, groups)
    grads, sides = lax.optimization_barrier((grads, sides))
    far = swapped(grads, "ja", 2)
    sides = lax.all_to_all(sides, "ia", 0, 0, tiled=True)
    near = swapped(grads, "ja", 1)
    farther = swapped(far, "ja", 1)
    products = triangle(sides, (grads, near, far, farther))
    products = lax.all_to_all(products, "ia", 0, 0, tiled=True)
    own, raw = gate(products, factors, normed, w)
    raw = raw + swapped(raw, "ja", 2)
    other = swapped(own, "col", 1)
    raw = raw + swapped(raw, "ja", 1)
    pieces = lax.all_to_all(raw.reshape(groups, -1, depth), "ia", 0, 0, tiled=True)
    piece = jnp.sum(pieces, axis=0)
    whole = lax.all_to_all(jnp.broadcast_to(piece[None], pieces.shape), "ia", 0, 0, tiled=True)
    whole = whole.reshape(4 * chans, depth)
    squares = jnp.sum(whole * whole).reshape(1, 1)
    others = swapped(squares, "col", 1)
    pair_grad = finish(unit, inv_std, norm_gain, own, other)
    others, pair_grad = lax.optimization_barrier((others, pair_grad))
    weight_grads = jnp.swapaxes(scale(whole, squares, others).reshape(4, chans, depth), 1, 2)
    return (pair_grad, weight_grads)


def solution(mesh):
    placed = (P("ia", "ja", None), P(), P(None, None, "col"), P(), P("ia", "col", "ja"))
    return jax.shard_map(
        on_device,
        mesh=mesh,
        in_specs=placed,
        out_specs=(P("ia", "ja", None), P(None, None, "col")),
        check_vma=False,
    )
```

time: 142 us -> 129 us (0.908)
  blocking collectives: 24.1 us -> 41.4 us
  waiting for transfers between devices: 57.2 us -> 44.2 us
  local copies, waits for them, and re-layouts: 13.8 us -> 2.04 us
  starting transfers between devices: 24.6 us -> 18.7 us
  Pallas kernels: 18.4 us -> 20.8 us
    all_to_all x0 -> x1, blocking collectives: none -> 19.1 us  [on_device(): products = lax.all_to_all(products, 'ia', 0, 0, tiled=True)]
    all_to_all x1 -> x0, waiting for transfers between devices: 16.4 us -> none  [on_device(): products = lax.all_to_all(products, 'ia', 0, 0, tiled=True)]
    unnamed x24 -> x6, local copies, waits for them, and re-layouts: 12.9 us -> 2.03 us
    all_to_all x1, waiting for transfers between devices: 0.01 us -> 4.49 us  [on_device(): grads = lax.all_to_all(grads, 'ia', 0, 0, tiled=True)]
    all_to_all x1 -> x0, starting transfers between devices: 3.66 us -> none  [on_device(): products = lax.all_to_all(products, 'ia', 0, 0, tiled=True)]
    all_to_all x1, starting transfers between devices: 7.17 us -> 3.66 us  [on_device(): sides = lax.all_to_all(sides, 'ia', 0, 0, tiled=True)]
    pallas_call x5 -> x6, Pallas kernels: 18.4 us -> 20.8 us  [call(): pl.pallas_call(kernel, grid=grid, out_shape=out_shape, in_specs=in_specs,...]
    all_to_all x1, waiting for transfers between devices: 11 us -> 8.93 us  [on_device(): sides = lax.all_to_all(sides, 'ia', 0, 0, tiled=True)]
  transfers between devices with their start and end apart: 10 -> 9, of which waited for: 6 -> 5; matrix products, arithmetic and copies ran while one was open for 1% -> 1% of each run, Pallas kernels for 7% -> 8%
where the time goes in v1:
time: 129 us; the launch traced here: 128 us
  waiting for transfers between devices  44.2 us (34%)
  blocking collectives  41.4 us (32%)
  Pallas kernels  20.8 us (16%)
  starting transfers between devices  18.7 us (14%)
  local copies, waits for them, and re-layouts  2.04 us (2%)
    ppermute x7, waiting for transfers between devices, swapped(): return lax.ppermute(x, axis, [(i, i ^ bit) for i in range(size)])  30.8 us
    pallas_call x6, Pallas kernels, call(): pl.pallas_call(kernel, grid=grid, out_shape=out_shape, in_specs=in_specs,...  20.8 us
    all_to_all x1, blocking collectives, on_device(): products = lax.all_to_all(products, 'ia', 0, 0, tiled=True)  19.1 us
    all_to_all x1, blocking collectives, on_device(): lax.all_to_all(raw.reshape(groups, -1, depth), 'ia', 0, 0, tiled=True)  11.2 us
    all_to_all x1, blocking collectives, on_device(): lax.all_to_all(jnp.broadcast_to(piece[None], pieces.shape), 'ia', 0, 0, t...  11.1 us
    all_to_all x1, waiting for transfers between devices, on_device(): sides = lax.all_to_all(sides, 'ia', 0, 0, tiled=True)  8.93 us
    ppermute x7, starting transfers between devices, swapped(): return lax.ppermute(x, axis, [(i, i ^ bit) for i in range(size)])  7.86 us
    all_to_all x1, starting transfers between devices, on_device(): grads = lax.all_to_all(grads, 'ia', 0, 0, tiled=True)  7.2 us
  transfers between devices with their start and end apart: 9, of which 5 were waited for; matrix products, arithmetic and copies ran while one was open for 1% of the time, Pallas kernels for 8%

profile of v1, /device:TPU:0, one launch (start us, length us, event | category | flops | bytes accessed | tf_op | source)
XLA Modules:
  0.0 128.5 jit_solution(15112615886058336786)
XLA Ops:
  0.6 1.0 copy-done
  1.7 1.4 %shard_map.68 = bf16[64,32,128]{2,1,0:T(8,128)(2,1)} custom-call(bf16[32,64,128]{2,1,0:T(8,128)(2,1)S(1)} %copy-done), custom_call_target="tpu_custom_call" | custom-call | flops 1000000 | bytes 1048576 | tf_op jit(solution)/shard_map/pallas_call | solution.py:38
  3.1 7.2 %all-to-all-start = ((bf16[16,4,32,128]{3,2,1,0:T(8,128)(2,1)}), bf16[16,4,32,128]{3,2,1,0:T(8,128)(2,1)}, u32[]{:S(2)}, u32[]{:S(2)}) async-start(bf16[16,4,32,128]{3,2,1,0:T(8,128)(2,1)} %bitcast), calls=%async_computation | async-start | bytes 1048576 | tf_op jit(solution)/shard_map/all_to_all | solution.py:290
  10.3 6.1 %shard_map.69 = (bf16[16,2,4,32,128]{4,3,2,1,0:T(8,128)(2,1)}, bf16[16,256,256]{2,1,0:T(8,128)(2,1)S(1)}, bf16[16,128,256]{2,1,0:T(8,128)(2,1)S(1)}, f32[16,128,256]{2,1,0:T(8,128)}, f32[16,1,256]{2,1,0:T(1,128)}) custom-call(bf16[32,128,128]{2,1,0:T(8,128)(2,1)} %refs_0_.1, f32[1,128]{1,0:T(1,128)} %bitcast.15, bf16[256,128]{1,0:T(8,128)(2,1)} %bitcast.17, ...), custom_call_target="tpu_custom_call" | custom-call | flops 6000000000 | bytes 8388608 | tf_op jit(solution)/shard_map/pallas_call | solution.py:38
  16.4 1.0 copy-done.1
  17.4 4.5 %all-to-all-done.refs_1_ = bf16[16,4,32,128]{3,2,1,0:T(8,128)(2,1)} async-done(((bf16[16,4,32,128]{3,2,1,0:T(8,128)(2,1)}), bf16[16,4,32,128]{3,2,1,0:T(8,128)(2,1)}, u32[]{:S(2)}, u32[]{:S(2)}) %all-to-all-start) | async-done | bytes 524320 | tf_op jit(solution)/shard_map/all_to_all | solution.py:290
  21.9 1.9 %collective-permute-start.1 = (bf16[16,4,32,128]{3,2,1,0:T(8,128)(2,1)}, bf16[16,4,32,128]{3,2,1,0:T(8,128)(2,1)}, u32[]{:S(2)}, u32[]{:S(2)}) collective-permute-start(bf16[16,4,32,128]{3,2,1,0:T(8,128)(2,1)} %all-to-all-done.refs_1_), channel_id=1, source_target_pairs={{0,4},{2,6},{4,0},{6,2},{1,5},{3,7},{5,1},{7,3},{8,12},{10,14},{12... | collective-permute-start | bytes 1572872 | tf_op jit(solution)/shard_map/ppermute | solution.py:279
  23.8 3.7 %all-to-all-start.1 = ((bf16[16,2,4,32,128]{4,3,2,1,0:T(8,128)(2,1)}), bf16[16,2,4,32,128]{4,3,2,1,0:T(8,128)(2,1)S(1)}, u32[]{:S(2)}, u32[]{:S(2)}) async-start(bf16[16,2,4,32,128]{4,3,2,1,0:T(8,128)(2,1)} %get-tuple-element.14), calls=%async_computation.1 | async-start | bytes 2097152 | tf_op jit(solution)/shard_map/all_to_all | solution.py:294
  27.4 0.1 collective-permute-start
  27.5 7.1 %collective-permute-done.1.refs_3_ = bf16[16,4,32,128]{3,2,1,0:T(8,128)(2,1)} collective-permute-done((bf16[16,4,32,128]{3,2,1,0:T(8,128)(2,1)}, bf16[16,4,32,128]{3,2,1,0:T(8,128)(2,1)}, u32[]{:S(2)}, u32[]{:S(2)}) %collective-permute-start.1) | collective-permute-done | bytes 524320 | tf_op jit(solution)/shard_map/ppermute | solution.py:279
  34.6 8.9 %all-to-all-done.1.refs_0_ = bf16[16,2,4,32,128]{4,3,2,1,0:T(8,128)(2,1)S(1)} async-done(((bf16[16,2,4,32,128]{4,3,2,1,0:T(8,128)(2,1)}), bf16[16,2,4,32,128]{4,3,2,1,0:T(8,128)(2,1)S(1)}, u32[]{:S(2)}, u32[]{:S(2)}) %all-to-all-start.1) | async-done | bytes 1048608 | tf_op jit(solution)/shard_map/all_to_all | solution.py:294
  43.6 3.8 %shard_map.70 = bf16[16,2,4,32,128]{4,3,2,1,0:T(8,128)(2,1)} custom-call(bf16[16,2,4,32,128]{4,3,2,1,0:T(8,128)(2,1)S(1)} %all-to-all-done.1.refs_0_, bf16[16,4,32,128]{3,2,1,0:T(8,128)(2,1)} %all-to-all-done.refs_1_, bf16[16,4,32,128]{3,2,1,0:T(8,128)(2,1)} %collective-permute-done.refs_2_, bf16[16,4,32,128]{3,2,1,0:T(8,128)(2,1)} %collective-permute-done.1.refs_3_, ...), custom_call_target="tpu_custom_call" | custom-call | flops 4000000000 | bytes 5242880 | tf_op jit(solution)/shard_map/pallas_call | solution.py:38
  47.3 19.1 %all_to_all.25.refs_0_ = bf16[16,2,4,32,128]{4,3,2,1,0:T(8,128)(2,1)S(1)} all-to-all(bf16[16,2,4,32,128]{4,3,2,1,0:T(8,128)(2,1)} %shard_map.70), channel_id=1, replica_groups=mesh['ia'=16,'ja'=4,'col'=2] {'ia'}, dimensions={0} | all-to-all | bytes 2097152 | tf_op jit(solution)/shard_map/all_to_all | solution.py:298
  66.4 3.7 %shard_map.71 = (bf16[16,128,256]{2,1,0:T(8,128)(2,1)}, f32[256,128]{1,0:T(8,128)S(1)}) custom-call(bf16[16,2,4,32,128]{4,3,2,1,0:T(8,128)(2,1)S(1)} %all_to_all.25.refs_0_, bf16[16,256,256]{2,1,0:T(8,128)(2,1)S(1)} %get-tuple-element.16.refs_1_, bf16[16,128,256]{2,1,0:T(8,128)(2,1)S(1)} %copy-done.2, bf16[256,128]{1,0:T(8,128)(2,1)} %bitcast.18), custom_call_target="tpu_custom_call" | custom-call | flops 6000000000 | bytes 8388608 | tf_op jit(solution)/shard_map/pallas_call | solution.py:38
  70.1 3.6 %collective-permute-start.6 = (bf16[16,128,256]{2,1,0:T(8,128)(2,1)}, bf16[16,128,256]{2,1,0:T(8,128)(2,1)S(1)}, u32[]{:S(2)}, u32[]{:S(2)}) collective-permute-start(bf16[16,128,256]{2,1,0:T(8,128)(2,1)} %get-tuple-element.21.own_ref), channel_id=1, source_target_pairs={{0,1},{1,0},{2,3},{3,2},{4,5},{5,4},{6,7},{7,6},{8,9},{9,8},{10,11... | collective-permute-start | bytes 3145736 | tf_op jit(solution)/shard_map/ppermute | solution.py:279
  73.7 22.3 %collective-permute-done.3 = f32[256,128]{1,0:T(8,128)S(1)} collective-permute-done((f32[256,128]{1,0:T(8,128)S(1)}, f32[256,128]{1,0:T(8,128)S(1)}, u32[]{:S(2)}, u32[]{:S(2)}) %collective-permute-start.3) | collective-permute-done | bytes 131104 | tf_op jit(solution)/shard_map/ppermute | solution.py:279
  96.1 0.1 collective-permute-start.4
  96.1 1.3 %collective-permute-done.4 = f32[256,128]{1,0:T(8,128)S(1)} collective-permute-done((f32[256,128]{1,0:T(8,128)S(1)}, f32[256,128]{1,0:T(8,128)S(1)}, u32[]{:S(2)}, u32[]{:S(2)}) %collective-permute-start.4) | collective-permute-done | bytes 131104 | tf_op jit(solution)/shard_map/ppermute | solution.py:279
  97.5 11.2 %all_to_all.26 = f32[16,16,128]{2,1,0:T(8,128)S(1)} all-to-all(f32[16,16,128]{2,1,0:T(8,128)S(1)} %bitcast.13), channel_id=1, replica_groups=mesh['ia'=16,'ja'=4,'col'=2] {'ia'}, dimensions={0} | all-to-all | bytes 262144 | tf_op jit(solution)/shard_map/all_to_all | solution.py:303
  108.8 11.1 %all_to_all.27 = f32[16,16,128]{2,1,0:T(8,128)S(1)} all-to-all(f32[16,16,128]{2,1,0:T(8,128)S(1)} %broadcast_in_dim.5), channel_id=1, replica_groups=mesh['ia'=16,'ja'=4,'col'=2] {'ia'}, dimensions={0} | all-to-all | bytes 262144 | tf_op jit(solution)/shard_map/all_to_all | solution.py:305
  119.8 0.6 multiply_reduce_fusion
  120.5 2.2 %collective-permute-start.5 = (f32[1,1]{1,0:T(1,128)}, f32[1,1]{1,0:T(1,128)}, u32[]{:S(2)}, u32[]{:S(2)}) collective-permute-start(f32[1,1]{1,0:T(1,128)} %bitcast.6.mine_ref), channel_id=1, source_target_pairs={{0,1},{1,0},{2,3},{3,2},{4,5},{5,4},{6,7},{7,6},{8,9},{9,8},{10,11... | collective-permute-start | bytes 20 | tf_op jit(solution)/shard_map/ppermute | solution.py:279
  122.6 3.9 %shard_map.72 = bf16[32,128,128]{2,1,0:T(8,128)(2,1)} custom-call(f32[16,128,256]{2,1,0:T(8,128)} %get-tuple-element.19.unit_ref, f32[16,1,256]{2,1,0:T(1,128)} %get-tuple-element.20.inv_ref, f32[1,128]{1,0:T(1,128)} %bitcast.16, bf16[16,128,256]{2,1,0:T(8,128)(2,1)} %get-tuple-element.21.own_ref, bf16[16,128,256]{2,1,0:T(8,128)(2,1)S(1)} %collective-permute-done.6.other_ref), custom_call_target="tpu_custom_call" | custom-call | flops 1000000000 | bytes 4194304 | tf_op jit(solution)/shard_map/pallas_call | solution.py:38
  126.5 1.9 %shard_map.73 = f32[256,128]{1,0:T(8,128)} custom-call(f32[256,128]{1,0:T(8,128)S(1)} %bitcast.12, f32[1,1]{1,0:T(1,128)} %bitcast.6.mine_ref, f32[1,1]{1,0:T(1,128)} %collective-permute-done.5.others_ref), custom_call_target="tpu_custom_call" | custom-call | flops 1000000 | bytes 1048576 | tf_op jit(solution)/shard_map/pallas_call | solution.py:38
  (14 shorter events, 0.1 us)
Async XLA Ops:
  0.6 1.0 copy-start
  3.1 18.8 %all-to-all-start = ((bf16[16,4,32,128]{3,2,1,0:T(8,128)(2,1)}), bf16[16,4,32,128]{3,2,1,0:T(8,128)(2,1)}, u32[]{:S(2)}, u32[]{:S(2)}) async-start(bf16[16,4,32,128]{3,2,1,0:T(8,128)(2,1)} %bitcast), calls=%async_computation | async-start | bytes 1048576 | tf_op jit(solution)/shard_map/all_to_all | solution.py:290
  16.4 1.0 copy-start.1
  21.9 12.8 %collective-permute-start.1 = (bf16[16,4,32,128]{3,2,1,0:T(8,128)(2,1)}, bf16[16,4,32,128]{3,2,1,0:T(8,128)(2,1)}, u32[]{:S(2)}, u32[]{:S(2)}) collective-permute-start(bf16[16,4,32,128]{3,2,1,0:T(8,128)(2,1)} %all-to-all-done.refs_1_), channel_id=1, source_target_pairs={{0,4},{2,6},{4,0},{6,2},{1,5},{3,7},{5,1},{7,3},{8,12},{10,14},{12... | collective-permute-start | bytes 1572872 | tf_op jit(solution)/shard_map/ppermute | solution.py:279
  23.8 19.8 %all-to-all-start.1 = ((bf16[16,2,4,32,128]{4,3,2,1,0:T(8,128)(2,1)}), bf16[16,2,4,32,128]{4,3,2,1,0:T(8,128)(2,1)S(1)}, u32[]{:S(2)}, u32[]{:S(2)}) async-start(bf16[16,2,4,32,128]{4,3,2,1,0:T(8,128)(2,1)} %get-tuple-element.14), calls=%async_computation.1 | async-start | bytes 2097152 | tf_op jit(solution)/shard_map/all_to_all | solution.py:294
  27.4 7.2 %collective-permute-start = (bf16[16,4,32,128]{3,2,1,0:T(8,128)(2,1)}, bf16[16,4,32,128]{3,2,1,0:T(8,128)(2,1)}, u32[]{:S(2)}, u32[]{:S(2)}) collective-permute-start(bf16[16,4,32,128]{3,2,1,0:T(8,128)(2,1)} %all-to-all-done.refs_1_), channel_id=1, source_target_pairs={{0,2},{2,0},{4,6},{6,4},{1,3},{3,1},{5,7},{7,5},{8,10},{10,8},{12,... | collective-permute-start | bytes 1572872 | tf_op jit(solution)/shard_map/ppermute | solution.py:279
  34.6 8.9 %collective-permute-start.2 = (bf16[16,4,32,128]{3,2,1,0:T(8,128)(2,1)}, bf16[16,4,32,128]{3,2,1,0:T(8,128)(2,1)}, u32[]{:S(2)}, u32[]{:S(2)}) collective-permute-start(bf16[16,4,32,128]{3,2,1,0:T(8,128)(2,1)} %collective-permute-done.1.refs_3_), channel_id=1, source_target_pairs={{0,2},{2,0},{4,6},{6,4},{1,3},{3,1},{5,7},{7,5},{8,10},{10,8},{12,... | collective-permute-start | bytes 1572872 | tf_op jit(solution)/shard_map/ppermute | solution.py:279
  47.3 19.1 %copy-start.2 = (bf16[16,128,256]{2,1,0:T(8,128)(2,1)S(1)}, bf16[16,128,256]{2,1,0:T(8,128)(2,1)}, u32[]{:S(2)}) copy-start(bf16[16,128,256]{2,1,0:T(8,128)(2,1)} %copy-done.1) | copy-start | bytes 3145732
  70.1 52.5 %collective-permute-start.6 = (bf16[16,128,256]{2,1,0:T(8,128)(2,1)}, bf16[16,128,256]{2,1,0:T(8,128)(2,1)S(1)}, u32[]{:S(2)}, u32[]{:S(2)}) collective-permute-start(bf16[16,128,256]{2,1,0:T(8,128)(2,1)} %get-tuple-element.21.own_ref), channel_id=1, source_target_pairs={{0,1},{1,0},{2,3},{3,2},{4,5},{5,4},{6,7},{7,6},{8,9},{9,8},{10,11... | collective-permute-start | bytes 3145736 | tf_op jit(solution)/shard_map/ppermute | solution.py:279
  73.7 22.4 %collective-permute-start.3 = (f32[256,128]{1,0:T(8,128)S(1)}, f32[256,128]{1,0:T(8,128)S(1)}, u32[]{:S(2)}, u32[]{:S(2)}) collective-permute-start(f32[256,128]{1,0:T(8,128)S(1)} %get-tuple-element.18), channel_id=1, source_target_pairs={{0,4},{2,6},{4,0},{6,2},{1,5},{3,7},{5,1},{7,3},{8,12},{10,14},{12... | collective-permute-start | bytes 393224 | tf_op jit(solution)/shard_map/ppermute | solution.py:279
  96.1 1.4 %collective-permute-start.4 = (f32[256,128]{1,0:T(8,128)S(1)}, f32[256,128]{1,0:T(8,128)S(1)}, u32[]{:S(2)}, u32[]{:S(2)}) collective-permute-start(f32[256,128]{1,0:T(8,128)S(1)} %add.6), channel_id=1, source_target_pairs={{0,2},{2,0},{4,6},{6,4},{1,3},{3,1},{5,7},{7,5},{8,10},{10,8},{12,... | collective-permute-start | bytes 393224 | tf_op jit(solution)/shard_map/ppermute | solution.py:279
  120.5 6.1 %collective-permute-start.5 = (f32[1,1]{1,0:T(1,128)}, f32[1,1]{1,0:T(1,128)}, u32[]{:S(2)}, u32[]{:S(2)}) collective-permute-start(f32[1,1]{1,0:T(1,128)} %bitcast.6.mine_ref), channel_id=1, source_target_pairs={{0,1},{1,0},{2,3},{3,2},{4,5},{5,4},{6,7},{7,6},{8,9},{9,8},{10,11... | collective-permute-start | bytes 20 | tf_op jit(solution)/shard_map/ppermute | solution.py:279

commit v2 on v1

--- a/solution.py
+++ b/solution.py
@@ -3,6 +3,7 @@
 from jax import lax
 from jax.experimental import pallas as pl
 from jax.experimental.pallas import tpu as pltpu
+from jax.sharding import Mesh
 from jax.sharding import PartitionSpec as P
 
 
@@ -99,7 +100,7 @@
         unit_ref[p] = unit
         inv_ref[p] = inv_std
         whole = step * (rows // 2) + p
-        normed_ref[whole] = normed
+        normed_ref[p] = normed
         proj = dot(w, normed)
         valid = jnp.concatenate([valid_cols * mask_ref[first_row + 2 * p + e].astype(F32) for e in range(2)], axis=1)
         for side in range(2):
@@ -123,7 +124,7 @@
                 sides_ref[g, side, c] = flat[pl.ds(first, rows, stride=2 * half), :].astype(BF)
 
 
-def project(x, gain, w, mask, groups, axes=("ia", "ja"), unroll=8, step=16):
+def project(x, gain, w, mask, groups, axes=("ia", ("z_lo", "core")), unroll=4, step=8):
     rows, cols, depth = x.shape
     half = w.shape[0] // 4
     per = half // groups
@@ -131,7 +132,7 @@
     out = [
         pltpu.HBM((groups, 2, per, rows, cols), BF),
         pltpu.VMEM((pairs, 4 * half, 2 * cols), BF),
-        pltpu.VMEM((pairs, depth, 2 * cols), BF),
+        pltpu.HBM((pairs, depth, 2 * cols), BF),
         pltpu.HBM((pairs, depth, 2 * cols), F32),
         pltpu.HBM((pairs, 1, 2 * cols), F32),
     ]
@@ -141,7 +142,7 @@
         out,
         [in_hbm(x), in_hbm(gain[None]), in_hbm(w), mask, in_hbm(table)],
         [leading(step, x.shape), fixed((1, depth)), fixed(w.shape), SCALARS, fixed(table.shape)],
-        [pl.BlockSpec((groups, 2, per, step, cols), lambda r: (0, 0, 0, r, 0))] + [KEPT, KEPT] + [leading(step // 2, o.shape) for o in out[3:]],
+        [pl.BlockSpec((groups, 2, per, step, cols), lambda r: (0, 0, 0, r, 0))] + [KEPT] + [leading(step // 2, o.shape) for o in out[2:]],
         [pltpu.VMEM((step * 2 * half, cols), F32), pltpu.VMEM((depth, 2 * cols), F32)],
         (rows // step,),
         flops=6 * 10**9,
@@ -168,7 +169,7 @@
         out_ref[:, 0, c] = total.astype(BF).reshape(groups, rows, cols)
 
 
-def triangle(sides, grads, axis="ja"):
+def triangle(sides, grads, axis=("z_lo", "core")):
     return call(
         lambda *refs: triangle_kernel(axis, *refs),
         pltpu.HBM(sides.shape, BF),
@@ -180,10 +181,10 @@
     )
 
 
-def gate_kernel(unroll, in_ref, factors_ref, normed_ref, w_ref, out_ref, raw_ref, flat):
+def gate_kernel(unroll, in_ref, factors_ref, normed_ref, w_ref, out_ref, raw_ref, flat, total):
     groups, _, per, rows, _ = in_ref.shape
     half = groups * per
-    pairs = out_ref.shape[0]
+    pairs = normed_ref.shape[0]
     step = pl.program_id(0)
 
     @pl.when(step == 0)
@@ -193,7 +194,7 @@
                 for c in range(per):
                     first = (side * half + g * per + c) * rows
                     flat[first : first + rows, :] = in_ref[g, side, c].astype(F32)
-        raw_ref[...] = jnp.zeros_like(raw_ref)
+        total[...] = jnp.zeros_like(total)
 
     w = w_ref[...].T
 
@@ -208,22 +209,26 @@
             for first in (at, at + half):
                 parts.append((incoming * factors_ref[p, first : first + half, :].astype(F32)).astype(BF))
         grads = jnp.concatenate(parts, axis=0)
-        raw_ref[...] += dot(grads, normed_ref[p], NT)
-        out_ref[q] = dot(w, grads).astype(BF)
+        total[...] += dot(grads, normed_ref[q], NT)
+        out_ref[p] = dot(w, grads).astype(BF)
         return carry
 
     lax.fori_loop(0, pairs, pair, 0, unroll=unroll)
 
-
-def gate(incoming, factors, normed, w, unroll=8, step=8):
+    @pl.when(step == pl.num_programs(0) - 1)
+    def _():
+        raw_ref[...] = total[...].astype(BF)
+
+
+def gate(incoming, factors, normed, w, unroll=4, step=4):
     groups, _, per, rows, cols = incoming.shape
     return call(
         lambda *refs: gate_kernel(unroll, *refs),
-        [pltpu.HBM(normed.shape, BF), jax.ShapeDtypeStruct(w.shape, F32)],
-        [kept(incoming), kept(factors), kept(normed), in_hbm(w)],
-        [KEPT, KEPT, KEPT, fixed(w.shape)],
-        [leading(step, normed.shape), fixed(w.shape)],
-        [pltpu.VMEM((2 * groups * per * rows, cols), F32)],
+        [pltpu.VMEM(normed.shape, BF), pltpu.VMEM(w.shape, BF)],
+        [kept(incoming), kept(factors), in_hbm(normed), in_hbm(w)],
+        [KEPT, KEPT, leading(step, normed.shape), fixed(w.shape)],
+        [KEPT, KEPT],
+        [pltpu.VMEM((2 * groups * per * rows, cols), F32), pltpu.VMEM(w.shape, F32)],
         (normed.shape[0] // step,),
         flops=6 * 10**9,
         moved=8 * MIB,
@@ -241,7 +246,7 @@
     base = pl.program_id(0) * (step // 2)
     for q in range(step // 2):
         unit = unit_ref[q]
-        scaled = (own_ref[q].astype(F32) + other_ref[base + q].astype(F32)) * gains[...]
+        scaled = (own_ref[base + q].astype(F32) + other_ref[base + q].astype(F32)) * gains[...]
         mean = jnp.mean(scaled, axis=0, keepdims=True)
         along = jnp.mean(scaled * unit, axis=0, keepdims=True)
         made = (inv_ref[q] * (scaled - mean - unit * along)).astype(BF)
@@ -255,8 +260,8 @@
     return call(
         finish_kernel,
         jax.ShapeDtypeStruct(shape, BF),
-        [in_hbm(unit), in_hbm(inv_std), in_hbm(gain[None]), in_hbm(own), kept(other)],
-        [leading(half, unit.shape), leading(half, inv_std.shape), fixed((1, depth)), leading(half, own.shape), KEPT],
+        [in_hbm(unit), in_hbm(inv_std), in_hbm(gain[None]), kept(own), kept(other)],
+        [leading(half, unit.shape), leading(half, inv_std.shape), fixed((1, depth)), KEPT, KEPT],
         leading(step, shape),
         [pltpu.VMEM((depth, twice), F32)],
         (shape[0] // step,),
@@ -265,18 +270,32 @@
     )
 
 
-def scale_kernel(whole_ref, mine_ref, others_ref, out_ref):
-    factor = jnp.minimum(1.0, CLIP_LIMIT * lax.rsqrt(mine_ref[...] + others_ref[...] + 1e-06))
-    out_ref[...] = whole_ref[...] * factor
-
-
-def scale(whole, mine, others):
-    return call(scale_kernel, pltpu.HBM(whole.shape, F32), [kept(whole), mine, others], [KEPT] * 3, KEPT)
-
-
-def swapped(x, axis, bit):
-    size = lax.axis_size(axis)
-    return lax.ppermute(x, axis, [(i, i ^ bit) for i in range(size)])
+def clip_kernel(axis, pieces_ref, out_ref):
+    count, rows, depth = pieces_ref.shape
+    here = lax.axis_index(axis)
+    total = jnp.zeros((rows, depth), F32)
+    for n in range(count):
+        piece = pieces_ref[n].astype(F32)
+        total = total + piece * piece
+    squares = jnp.sum(jnp.sum(total, axis=0, keepdims=True), axis=1, keepdims=True)
+    factor = jnp.minimum(1.0, CLIP_LIMIT * lax.rsqrt(squares + 1e-06))
+    for n in range(count // 2):
+        out_ref[n * rows : (n + 1) * rows, :] = pieces_ref[2 * n + here].astype(F32) * factor
+
+
+def clip(pieces, axis="col"):
+    count, rows, depth = pieces.shape
+    return call(
+        lambda *refs: clip_kernel(axis, *refs),
+        pltpu.HBM((count // 2 * rows, depth), F32),
+        [kept(pieces)],
+        [KEPT],
+        KEPT,
+    )
+
+
+def swapped(x, axis):
+    return lax.ppermute(x, axis, [(0, 1), (1, 0)])
 
 
 def on_device(pair_rep, norm_gain, weights, residue_mask, product_grad):
@@ -290,34 +309,36 @@
     grads = lax.all_to_all(grads, "ia", 0, 0, tiled=True)
     sides, factors, normed, unit, inv_std = project(pair_rep, norm_gain, w, residue_mask, groups)
     grads, sides = lax.optimization_barrier((grads, sides))
-    far = swapped(grads, "ja", 2)
+    far = swapped(grads, "z_lo")
     sides = lax.all_to_all(sides, "ia", 0, 0, tiled=True)
-    near = swapped(grads, "ja", 1)
-    farther = swapped(far, "ja", 1)
+    near = swapped(grads, "core")
+    farther = swapped(far, "core")
     products = triangle(sides, (grads, near, far, farther))
     products = lax.all_to_all(products, "ia", 0, 0, tiled=True)
     own, raw = gate(products, factors, normed, w)
-    raw = raw + swapped(raw, "ja", 2)
-    other = swapped(own, "col", 1)
-    raw = raw + swapped(raw, "ja", 1)
-    pieces = lax.all_to_all(raw.reshape(groups, -1, depth), "ia", 0, 0, tiled=True)
-    piece = jnp.sum(pieces, axis=0)
-    whole = lax.all_to_all(jnp.broadcast_to(piece[None], pieces.shape), "ia", 0, 0, tiled=True)
-    whole = whole.reshape(4 * chans, depth)
-    squares = jnp.sum(whole * whole).reshape(1, 1)
-    others = swapped(squares, "col", 1)
+    raw = raw.astype(F32) + swapped(raw, "z_lo").astype(F32)
+    other = swapped(own, "col")
+    peers = ("ia", "core")
+    pieces = raw.reshape(lax.axis_size(peers), -1, depth)
+    piece = jnp.sum(lax.all_to_all(pieces, peers, 0, 0, tiled=True), axis=0)
+    everyone = ("ia", "core", "col")
+    copies = jnp.broadcast_to(piece.astype(BF)[None], (lax.axis_size(everyone),) + piece.shape)
+    pieces = lax.all_to_all(copies, everyone, 0, 0, tiled=True)
     pair_grad = finish(unit, inv_std, norm_gain, own, other)
-    others, pair_grad = lax.optimization_barrier((others, pair_grad))
-    weight_grads = jnp.swapaxes(scale(whole, squares, others).reshape(4, chans, depth), 1, 2)
+    pieces, pair_grad = lax.optimization_barrier((pieces, pair_grad))
+    weight_grads = jnp.swapaxes(clip(pieces).reshape(4, chans, depth), 1, 2)
     return (pair_grad, weight_grads)
 
 
 def solution(mesh):
-    placed = (P("ia", "ja", None), P(), P(None, None, "col"), P(), P("ia", "col", "ja"))
+    sizes = dict(mesh.shape)
+    split = (sizes["ia"], sizes["ja"] // 2, 2, sizes["col"])
+    fine = Mesh(mesh.devices.reshape(split), ("ia", "z_lo", "core", "col"))
+    ja = ("z_lo", "core")
     return jax.shard_map(
         on_device,
-        mesh=mesh,
-        in_specs=placed,
-        out_specs=(P("ia", "ja", None), P(None, None, "col")),
+        mesh=fine,
+        in_specs=(P("ia", ja, None), P(), P(None, None, "col"), P(), P("ia", "col", ja)),
+        out_specs=(P("ia", ja, None), P(None, None, "col")),
         check_vma=False,
     )

time: 129 us -> 125 us (0.969); the launches traced: 128 us -> 123 us
  blocking collectives: 41.4 us -> 30.2 us
  waiting for transfers between devices: 44.2 us -> 48.6 us
  starting transfers between devices: 18.7 us -> 22.5 us
  Pallas kernels: 20.8 us -> 19.3 us
    all_to_all x2 -> x1, blocking collectives: 22.3 us -> 11.3 us  [on_device(): piece = jnp.sum(lax.all_to_all(pieces, peers, 0, 0, tiled=True), axis=0)]
    all_to_all x0 -> x1, waiting for transfers between devices: none -> 6.1 us  [on_device(): pieces = lax.all_to_all(copies, everyone, 0, 0, tiled=True)]
    all_to_all x0 -> x1, starting transfers between devices: none -> 6.01 us  [on_device(): pieces = lax.all_to_all(copies, everyone, 0, 0, tiled=True)]
    ppermute x7 -> x5, waiting for transfers between devices: 30.8 us -> 27.8 us  [swapped(): return lax.ppermute(x, axis, [(0, 1), (1, 0)])]
    ppermute x7 -> x5, starting transfers between devices: 7.86 us -> 5.67 us  [swapped(): return lax.ppermute(x, axis, [(0, 1), (1, 0)])]
    pallas_call x6, Pallas kernels: 20.8 us -> 19.3 us  [call(): pl.pallas_call(kernel, grid=grid, out_shape=out_shape, in_specs=in_specs,...]
  transfers between devices with their start and end apart: 9 -> 8, of which waited for: 5 -> 5; matrix products, arithmetic and copies ran while one was open for 1% -> 1% of each run, Pallas kernels for 8% -> 8%
where the time goes in v2:
time: 125 us; the launch traced here: 123 us
  waiting for transfers between devices  48.6 us (39%)
  blocking collectives  30.2 us (24%)
  starting transfers between devices  22.5 us (18%)
  Pallas kernels  19.3 us (15%)
  local copies, waits for them, and re-layouts  1.71 us (1%)
    ppermute x5, waiting for transfers between devices, swapped(): return lax.ppermute(x, axis, [(0, 1), (1, 0)])  27.8 us
    pallas_call x6, Pallas kernels, call(): pl.pallas_call(kernel, grid=grid, out_shape=out_shape, in_specs=in_specs,...  19.3 us
    all_to_all x1, blocking collectives, on_device(): products = lax.all_to_all(products, 'ia', 0, 0, tiled=True)  18.9 us
    all_to_all x1, blocking collectives, on_device(): piece = jnp.sum(lax.all_to_all(pieces, peers, 0, 0, tiled=True), axis=0)  11.3 us
    all_to_all x1, waiting for transfers between devices, on_device(): sides = lax.all_to_all(sides, 'ia', 0, 0, tiled=True)  8.93 us
    all_to_all x1, starting transfers between devices, on_device(): grads = lax.all_to_all(grads, 'ia', 0, 0, tiled=True)  7.2 us
    all_to_all x1, waiting for transfers between devices, on_device(): pieces = lax.all_to_all(copies, everyone, 0, 0, tiled=True)  6.1 us
    all_to_all x1, starting transfers between devices, on_device(): pieces = lax.all_to_all(copies, everyone, 0, 0, tiled=True)  6.01 us
  transfers between devices with their start and end apart: 8, of which 5 were waited for; matrix products, arithmetic and copies ran while one was open for 1% of the time, Pallas kernels for 8%

profile of v2, /device:TPU:0, one launch (start us, length us, event | category | flops | bytes accessed | tf_op | source)
XLA Modules:
  0.0 123.1 jit_solution(18093439526627869394)
XLA Ops:
  0.6 1.0 copy-done
  1.7 1.4 %shard_map.68 = bf16[64,32,128]{2,1,0:T(8,128)(2,1)} custom-call(bf16[32,64,128]{2,1,0:T(8,128)(2,1)S(1)} %copy-done), custom_call_target="tpu_custom_call" | custom-call | flops 1000000 | bytes 1048576 | tf_op jit(solution)/shard_map/pallas_call | solution.py:39
  3.1 7.2 %all-to-all-start = ((bf16[16,4,32,128]{3,2,1,0:T(8,128)(2,1)}), bf16[16,4,32,128]{3,2,1,0:T(8,128)(2,1)}, u32[]{:S(2)}, u32[]{:S(2)}) async-start(bf16[16,4,32,128]{3,2,1,0:T(8,128)(2,1)} %bitcast), calls=%async_computation | async-start | bytes 1048576 | tf_op jit(solution)/shard_map/all_to_all | solution.py:309
  10.3 5.8 %shard_map.69 = (bf16[16,2,4,32,128]{4,3,2,1,0:T(8,128)(2,1)}, bf16[16,256,256]{2,1,0:T(8,128)(2,1)S(1)}, bf16[16,128,256]{2,1,0:T(8,128)(2,1)}, f32[16,128,256]{2,1,0:T(8,128)}, f32[16,1,256]{2,1,0:T(1,128)}) custom-call(bf16[32,128,128]{2,1,0:T(8,128)(2,1)} %refs_0_.1, f32[1,128]{1,0:T(1,128)} %bitcast.12, bf16[256,128]{1,0:T(8,128)(2,1)} %bitcast.14, ...), custom_call_target="tpu_custom_call" | custom-call | flops 6000000000 | bytes 8388608 | tf_op jit(solution)/shard_map/pallas_call | solution.py:39
  16.1 5.8 %all-to-all-done.refs_1_ = bf16[16,4,32,128]{3,2,1,0:T(8,128)(2,1)} async-done(((bf16[16,4,32,128]{3,2,1,0:T(8,128)(2,1)}), bf16[16,4,32,128]{3,2,1,0:T(8,128)(2,1)}, u32[]{:S(2)}, u32[]{:S(2)}) %all-to-all-start) | async-done | bytes 524320 | tf_op jit(solution)/shard_map/all_to_all | solution.py:309
  21.9 1.9 %collective-permute-start.1 = (bf16[16,4,32,128]{3,2,1,0:T(8,128)(2,1)}, bf16[16,4,32,128]{3,2,1,0:T(8,128)(2,1)}, u32[]{:S(2)}, u32[]{:S(2)}) collective-permute-start(bf16[16,4,32,128]{3,2,1,0:T(8,128)(2,1)} %all-to-all-done.refs_1_), channel_id=1, source_target_pairs={{0,4},{4,0},{1,5},{5,1},{2,6},{6,2},{3,7},{7,3},{8,12},{12,8},{9,1... | collective-permute-start | bytes 1572872 | tf_op jit(solution)/shard_map/ppermute | solution.py:298
  23.8 3.7 %all-to-all-start.1 = ((bf16[16,2,4,32,128]{4,3,2,1,0:T(8,128)(2,1)}), bf16[16,2,4,32,128]{4,3,2,1,0:T(8,128)(2,1)S(1)}, u32[]{:S(2)}, u32[]{:S(2)}) async-start(bf16[16,2,4,32,128]{4,3,2,1,0:T(8,128)(2,1)} %get-tuple-element.14), calls=%async_computation.1 | async-start | bytes 2097152 | tf_op jit(solution)/shard_map/all_to_all | solution.py:313
  27.4 0.1 collective-permute-start
  27.5 7.1 %collective-permute-done.1.refs_3_ = bf16[16,4,32,128]{3,2,1,0:T(8,128)(2,1)} collective-permute-done((bf16[16,4,32,128]{3,2,1,0:T(8,128)(2,1)}, bf16[16,4,32,128]{3,2,1,0:T(8,128)(2,1)}, u32[]{:S(2)}, u32[]{:S(2)}) %collective-permute-start.1) | collective-permute-done | bytes 524320 | tf_op jit(solution)/shard_map/ppermute | solution.py:298
  34.6 0.0 collective-permute-start.2
  34.6 0.0 collective-permute-done.refs_2_
  34.6 8.9 %all-to-all-done.1.refs_0_ = bf16[16,2,4,32,128]{4,3,2,1,0:T(8,128)(2,1)S(1)} async-done(((bf16[16,2,4,32,128]{4,3,2,1,0:T(8,128)(2,1)}), bf16[16,2,4,32,128]{4,3,2,1,0:T(8,128)(2,1)S(1)}, u32[]{:S(2)}, u32[]{:S(2)}) %all-to-all-start.1) | async-done | bytes 1048608 | tf_op jit(solution)/shard_map/all_to_all | solution.py:313
  43.6 3.8 %shard_map.70 = bf16[16,2,4,32,128]{4,3,2,1,0:T(8,128)(2,1)} custom-call(bf16[16,2,4,32,128]{4,3,2,1,0:T(8,128)(2,1)S(1)} %all-to-all-done.1.refs_0_, bf16[16,4,32,128]{3,2,1,0:T(8,128)(2,1)} %all-to-all-done.refs_1_, bf16[16,4,32,128]{3,2,1,0:T(8,128)(2,1)} %collective-permute-done.refs_2_, bf16[16,4,32,128]{3,2,1,0:T(8,128)(2,1)} %collective-permute-done.1.refs_3_, ...), custom_call_target="tpu_custom_call" | custom-call | flops 4000000000 | bytes 5242880 | tf_op jit(solution)/shard_map/pallas_call | solution.py:39
  47.3 18.9 %all_to_all.25.refs_0_ = bf16[16,2,4,32,128]{4,3,2,1,0:T(8,128)(2,1)S(1)} all-to-all(bf16[16,2,4,32,128]{4,3,2,1,0:T(8,128)(2,1)} %shard_map.70), channel_id=1, replica_groups=mesh['ia'=16,'z_lo'=2,'core'=2,'col'=2] {'ia'}, dimensions={0} | all-to-all | bytes 2097152 | tf_op jit(solution)/shard_map/all_to_all | solution.py:317
  66.3 3.7 %shard_map.71 = (bf16[16,128,256]{2,1,0:T(8,128)(2,1)S(1)}, bf16[256,128]{1,0:T(8,128)(2,1)S(1)}) custom-call(bf16[16,2,4,32,128]{4,3,2,1,0:T(8,128)(2,1)S(1)} %all_to_all.25.refs_0_, bf16[16,256,256]{2,1,0:T(8,128)(2,1)S(1)} %get-tuple-element.16.refs_1_, bf16[16,128,256]{2,1,0:T(8,128)(2,1)} %get-tuple-element.17.refs_2_, bf16[256,128]{1,0:T(8,128)(2,1)} %bitcast.15), custom_call_target="tpu_custom_call" | custom-call | flops 6000000000 | bytes 8388608 | tf_op jit(solution)/shard_map/pallas_call | solution.py:39
  70.0 3.7 %collective-permute-start.4 = (bf16[16,128,256]{2,1,0:T(8,128)(2,1)S(1)}, bf16[16,128,256]{2,1,0:T(8,128)(2,1)S(1)}, u32[]{:S(2)}, u32[]{:S(2)}) collective-permute-start(bf16[16,128,256]{2,1,0:T(8,128)(2,1)S(1)} %get-tuple-element.21.own_ref), channel_id=1, source_target_pairs={{0,1},{1,0},{2,3},{3,2},{4,5},{5,4},{6,7},{7,6},{8,9},{9,8},{10,11... | collective-permute-start | bytes 3145736 | tf_op jit(solution)/shard_map/ppermute | solution.py:298
  73.7 0.0 collective-permute-start.3
  73.7 20.7 %collective-permute-done.3 = bf16[256,128]{1,0:T(8,128)(2,1)S(1)} collective-permute-done((bf16[256,128]{1,0:T(8,128)(2,1)S(1)}, bf16[256,128]{1,0:T(8,128)(2,1)S(1)}, u32[]{:S(2)}, u32[]{:S(2)}) %collective-permute-start.3) | collective-permute-done | bytes 65568 | tf_op jit(solution)/shard_map/ppermute | solution.py:298
  94.4 11.3 %all_to_all.26 = f32[32,8,128]{2,1,0:T(8,128)S(1)} all-to-all(f32[32,8,128]{2,1,0:T(8,128)S(1)} %add_bitcast_fusion), channel_id=1, replica_groups=mesh['ia'=16,'z_lo'=2,'core'=2,'col'=2] {'ia','core'}, dimensions={0} | all-to-all | bytes 262144 | tf_op jit(solution)/shard_map/all_to_all | solution.py:323
  105.7 0.7 broadcast_in_dim.5
  106.4 6.0 %all-to-all-start.4 = ((bf16[64,8,128]{2,1,0:T(8,128)(2,1)}), bf16[64,8,128]{2,1,0:T(8,128)(2,1)S(1)}, u32[]{:S(2)}, u32[]{:S(2)}) async-start(bf16[64,8,128]{2,1,0:T(8,128)(2,1)} %broadcast_in_dim.5), calls=%async_computation.4 | async-start | bytes 262144 | tf_op jit(solution)/shard_map/all_to_all | solution.py:326
  112.4 3.8 %shard_map.72 = bf16[32,128,128]{2,1,0:T(8,128)(2,1)} custom-call(f32[16,128,256]{2,1,0:T(8,128)} %get-tuple-element.19.unit_ref, f32[16,1,256]{2,1,0:T(1,128)} %get-tuple-element.20.inv_ref, f32[1,128]{1,0:T(1,128)} %bitcast.13, bf16[16,128,256]{2,1,0:T(8,128)(2,1)S(1)} %get-tuple-element.21.own_ref, bf16[16,128,256]{2,1,0:T(8,128)(2,1)S(1)} %collective-permute-done.4.other_ref), custom_call_target="tpu_custom_call" | custom-call | flops 1000000000 | bytes 4194304 | tf_op jit(solution)/shard_map/pallas_call | solution.py:39
  116.2 6.1 %all-to-all-done.4.refs_0_ = bf16[64,8,128]{2,1,0:T(8,128)(2,1)S(1)} async-done(((bf16[64,8,128]{2,1,0:T(8,128)(2,1)}), bf16[64,8,128]{2,1,0:T(8,128)(2,1)S(1)}, u32[]{:S(2)}, u32[]{:S(2)}) %all-to-all-start.4) | async-done | bytes 131104 | tf_op jit(solution)/shard_map/all_to_all | solution.py:326
  122.3 0.8 shard_map.73
  (5 shorter events, 0.1 us)
Async XLA Ops:
  0.6 1.0 copy-start
  3.1 18.8 %all-to-all-start = ((bf16[16,4,32,128]{3,2,1,0:T(8,128)(2,1)}), bf16[16,4,32,128]{3,2,1,0:T(8,128)(2,1)}, u32[]{:S(2)}, u32[]{:S(2)}) async-start(bf16[16,4,32,128]{3,2,1,0:T(8,128)(2,1)} %bitcast), calls=%async_computation | async-start | bytes 1048576 | tf_op jit(solution)/shard_map/all_to_all | solution.py:309
  21.9 12.8 %collective-permute-start.1 = (bf16[16,4,32,128]{3,2,1,0:T(8,128)(2,1)}, bf16[16,4,32,128]{3,2,1,0:T(8,128)(2,1)}, u32[]{:S(2)}, u32[]{:S(2)}) collective-permute-start(bf16[16,4,32,128]{3,2,1,0:T(8,128)(2,1)} %all-to-all-done.refs_1_), channel_id=1, source_target_pairs={{0,4},{4,0},{1,5},{5,1},{2,6},{6,2},{3,7},{7,3},{8,12},{12,8},{9,1... | collective-permute-start | bytes 1572872 | tf_op jit(solution)/shard_map/ppermute | solution.py:298
  23.8 19.8 %all-to-all-start.1 = ((bf16[16,2,4,32,128]{4,3,2,1,0:T(8,128)(2,1)}), bf16[16,2,4,32,128]{4,3,2,1,0:T(8,128)(2,1)S(1)}, u32[]{:S(2)}, u32[]{:S(2)}) async-start(bf16[16,2,4,32,128]{4,3,2,1,0:T(8,128)(2,1)} %get-tuple-element.14), calls=%async_computation.1 | async-start | bytes 2097152 | tf_op jit(solution)/shard_map/all_to_all | solution.py:313
  27.4 7.2 %collective-permute-start = (bf16[16,4,32,128]{3,2,1,0:T(8,128)(2,1)}, bf16[16,4,32,128]{3,2,1,0:T(8,128)(2,1)}, u32[]{:S(2)}, u32[]{:S(2)}) collective-permute-start(bf16[16,4,32,128]{3,2,1,0:T(8,128)(2,1)} %all-to-all-done.refs_1_), channel_id=1, source_target_pairs={{0,2},{2,0},{1,3},{3,1},{4,6},{6,4},{5,7},{7,5},{8,10},{10,8},{9,1... | collective-permute-start | bytes 1572872 | tf_op jit(solution)/shard_map/ppermute | solution.py:298
  34.6 8.9 %collective-permute-start.2 = (bf16[16,4,32,128]{3,2,1,0:T(8,128)(2,1)}, bf16[16,4,32,128]{3,2,1,0:T(8,128)(2,1)}, u32[]{:S(2)}, u32[]{:S(2)}) collective-permute-start(bf16[16,4,32,128]{3,2,1,0:T(8,128)(2,1)} %collective-permute-done.1.refs_3_), channel_id=1, source_target_pairs={{0,2},{2,0},{1,3},{3,1},{4,6},{6,4},{5,7},{7,5},{8,10},{10,8},{9,1... | collective-permute-start | bytes 1572872 | tf_op jit(solution)/shard_map/ppermute | solution.py:298
  70.0 42.4 %collective-permute-start.4 = (bf16[16,128,256]{2,1,0:T(8,128)(2,1)S(1)}, bf16[16,128,256]{2,1,0:T(8,128)(2,1)S(1)}, u32[]{:S(2)}, u32[]{:S(2)}) collective-permute-start(bf16[16,128,256]{2,1,0:T(8,128)(2,1)S(1)} %get-tuple-element.21.own_ref), channel_id=1, source_target_pairs={{0,1},{1,0},{2,3},{3,2},{4,5},{5,4},{6,7},{7,6},{8,9},{9,8},{10,11... | collective-permute-start | bytes 3145736 | tf_op jit(solution)/shard_map/ppermute | solution.py:298
  73.7 20.7 %collective-permute-start.3 = (bf16[256,128]{1,0:T(8,128)(2,1)S(1)}, bf16[256,128]{1,0:T(8,128)(2,1)S(1)}, u32[]{:S(2)}, u32[]{:S(2)}) collective-permute-start(bf16[256,128]{1,0:T(8,128)(2,1)S(1)} %get-tuple-element.18), channel_id=1, source_target_pairs={{0,4},{4,0},{1,5},{5,1},{2,6},{6,2},{3,7},{7,3},{8,12},{12,8},{9,1... | collective-permute-start | bytes 196616 | tf_op jit(solution)/shard_map/ppermute | solution.py:298
  106.4 15.9 %all-to-all-start.4 = ((bf16[64,8,128]{2,1,0:T(8,128)(2,1)}), bf16[64,8,128]{2,1,0:T(8,128)(2,1)S(1)}, u32[]{:S(2)}, u32[]{:S(2)}) async-start(bf16[64,8,128]{2,1,0:T(8,128)(2,1)} %broadcast_in_dim.5), calls=%async_computation.4 | async-start | bytes 262144 | tf_op jit(solution)/shard_map/all_to_all | solution.py:326

commit v3 on v2

--- a/solution.py
+++ b/solution.py
@@ -99,7 +99,6 @@
         normed = (unit * gains[...]).astype(BF)
         unit_ref[p] = unit
         inv_ref[p] = inv_std
-        whole = step * (rows // 2) + p
         normed_ref[p] = normed
         proj = dot(w, normed)
         valid = jnp.concatenate([valid_cols * mask_ref[first_row + 2 * p + e].astype(F32) for e in range(2)], axis=1)
@@ -112,8 +111,8 @@
             for e in range(2):
                 put = pl.multiple_of((2 * p + e) * 2 * half + side * half, half)
                 flat[pl.ds(put, half), :] = both[:, e * cols : (e + 1) * cols]
-            factors_ref[whole, at : at + half, :] = first.astype(BF)
-            factors_ref[whole, at + half : at + 2 * half, :] = (both * (1.0 - gate)).astype(BF)
+            factors_ref[p, at : at + half, :] = first.astype(BF)
+            factors_ref[p, at + half : at + 2 * half, :] = (both * (1.0 - gate)).astype(BF)
         return carry
 
     lax.fori_loop(0, rows // 2, pair, 0, unroll=unroll)
@@ -131,7 +130,7 @@
     pairs = rows // 2
     out = [
         pltpu.HBM((groups, 2, per, rows, cols), BF),
-        pltpu.VMEM((pairs, 4 * half, 2 * cols), BF),
+        pltpu.HBM((pairs, 4 * half, 2 * cols), BF),
         pltpu.HBM((pairs, depth, 2 * cols), BF),
         pltpu.HBM((pairs, depth, 2 * cols), F32),
         pltpu.HBM((pairs, 1, 2 * cols), F32),
@@ -142,7 +141,7 @@
         out,
         [in_hbm(x), in_hbm(gain[None]), in_hbm(w), mask, in_hbm(table)],
         [leading(step, x.shape), fixed((1, depth)), fixed(w.shape), SCALARS, fixed(table.shape)],
-        [pl.BlockSpec((groups, 2, per, step, cols), lambda r: (0, 0, 0, r, 0))] + [KEPT] + [leading(step // 2, o.shape) for o in out[2:]],
+        [pl.BlockSpec((groups, 2, per, step, cols), lambda r: (0, 0, 0, r, 0))] + [leading(step // 2, o.shape) for o in out[1:]],
         [pltpu.VMEM((step * 2 * half, cols), F32), pltpu.VMEM((depth, 2 * cols), F32)],
         (rows // step,),
         flops=6 * 10**9,
@@ -152,30 +151,33 @@
 
 def triangle_kernel(axis, sides_ref, *refs):
     *grads, out_ref = refs
-    groups, _, per, rows, cols = sides_ref.shape
+    groups, _, _, rows, cols = sides_ref.shape
     share = groups // len(grads)
     here = lax.axis_index(axis)
-    for c in range(per):
-        left = sides_ref[:, 0, c].reshape(groups * rows, cols)
-        total = None
-        for t, grad_ref in enumerate(grads):
-            first = (here ^ t) * share
-            grad = grad_ref[:, c].reshape(groups * rows, cols)
-            right = sides_ref[pl.ds(first, share), 1, c].reshape(share * rows, cols)
-            part = dot(grad, right)
-            total = part if total is None else total + part
-            back = dot(grad, left, TN)
-            out_ref[pl.ds(first, share), 1, c] = back.astype(BF).reshape(share, rows, cols)
-        out_ref[:, 0, c] = total.astype(BF).reshape(groups, rows, cols)
+    c = pl.program_id(0)
+    left = sides_ref[:, 0, c].reshape(groups * rows, cols)
+    total = None
+    for t, grad_ref in enumerate(grads):
+        first = (here ^ t) * share
+        grad = grad_ref[:, 0].reshape(groups * rows, cols)
+        right = sides_ref[pl.ds(first, share), 1, c].reshape(share * rows, cols)
+        part = dot(grad, right)
+        total = part if total is None else total + part
+        back = dot(grad, left, TN)
+        out_ref[pl.ds(first, share), 1, 0] = back.astype(BF).reshape(share, rows, cols)
+    out_ref[:, 0, 0] = total.astype(BF).reshape(groups, rows, cols)
 
 
 def triangle(sides, grads, axis=("z_lo", "core")):
+    groups, _, per, rows, cols = sides.shape
+    grad_spec = pl.BlockSpec((groups, 1, rows, cols), lambda c: (0, c, 0, 0))
     return call(
         lambda *refs: triangle_kernel(axis, *refs),
-        pltpu.HBM(sides.shape, BF),
-        [kept(sides)] + [in_hbm(g) for g in grads],
-        [KEPT] * (1 + len(grads)),
-        KEPT,
+        pltpu.VMEM(sides.shape, BF),
+        [kept(sides)] + [kept(g) for g in grads],
+        [KEPT] + [grad_spec] * len(grads),
+        pl.BlockSpec((groups, 2, 1, rows, cols), lambda c: (0, 0, c, 0, 0)),
+        grid=(per,),
         flops=4 * 10**9,
         moved=5 * MIB,
     )
@@ -207,10 +209,10 @@
             )
             at = 2 * side * half
             for first in (at, at + half):
-                parts.append((incoming * factors_ref[p, first : first + half, :].astype(F32)).astype(BF))
+                parts.append((incoming * factors_ref[q, first : first + half, :].astype(F32)).astype(BF))
         grads = jnp.concatenate(parts, axis=0)
         total[...] += dot(grads, normed_ref[q], NT)
-        out_ref[p] = dot(w, grads).astype(BF)
+        out_ref[q] = dot(w, grads).astype(BF)
         return carry
 
     lax.fori_loop(0, pairs, pair, 0, unroll=unroll)
@@ -220,14 +222,14 @@
         raw_ref[...] = total[...].astype(BF)
 
 
-def gate(incoming, factors, normed, w, unroll=4, step=4):
+def gate(incoming, factors, normed, w, unroll=8, step=8):
     groups, _, per, rows, cols = incoming.shape
     return call(
         lambda *refs: gate_kernel(unroll, *refs),
         [pltpu.VMEM(normed.shape, BF), pltpu.VMEM(w.shape, BF)],
-        [kept(incoming), kept(factors), in_hbm(normed), in_hbm(w)],
-        [KEPT, KEPT, leading(step, normed.shape), fixed(w.shape)],
-        [KEPT, KEPT],
+        [kept(incoming), in_hbm(factors), in_hbm(normed), in_hbm(w)],
+        [KEPT, leading(step, factors.shape), leading(step, normed.shape), fixed(w.shape)],
+        [leading(step, normed.shape), fixed(w.shape)],
         [pltpu.VMEM((2 * groups * per * rows, cols), F32), pltpu.VMEM(w.shape, F32)],
         (normed.shape[0] // step,),
         flops=6 * 10**9,
@@ -268,6 +270,21 @@
         flops=10**9,
         moved=4 * MIB,
     )
+
+
+def gather_kernel(pieces_ref, out_ref):
+    count, _, _ = pieces_ref.shape
+    total = pieces_ref[0]
+    for n in range(1, count):
+        total = total + pieces_ref[n]
+    piece = total.astype(BF)
+    for n in range(out_ref.shape[0]):
+        out_ref[n] = piece
+
+
+def summed_copies(pieces, count):
+    out = pltpu.HBM((count,) + pieces.shape[1:], BF)
+    return call(gather_kernel, out, [kept(pieces)], [KEPT], KEPT)
 
 
 def clip_kernel(axis, pieces_ref, out_ref):
@@ -320,9 +337,9 @@
     other = swapped(own, "col")
     peers = ("ia", "core")
     pieces = raw.reshape(lax.axis_size(peers), -1, depth)
-    piece = jnp.sum(lax.all_to_all(pieces, peers, 0, 0, tiled=True), axis=0)
+    pieces = lax.all_to_all(pieces, peers, 0, 0, tiled=True)
     everyone = ("ia", "core", "col")
-    copies = jnp.broadcast_to(piece.astype(BF)[None], (lax.axis_size(everyone),) + piece.shape)
+    copies = summed_copies(pieces, lax.axis_size(everyone))
     pieces = lax.all_to_all(copies, everyone, 0, 0, tiled=True)
     pair_grad = finish(unit, inv_std, norm_gain, own, other)
     pieces, pair_grad = lax.optimization_barrier((pieces, pair_grad))

time: 125 us -> 122 us (0.976)
    pallas_call x6 -> x7, Pallas kernels: 19.3 us -> 18.5 us  [call(): pl.pallas_call(kernel, grid=grid, out_shape=out_shape, in_specs=in_specs,...]
  transfers between devices with their start and end apart: 8 -> 8, of which waited for: 5 -> 5; matrix products, arithmetic and copies ran while one was open for 1% -> 0% of each run, Pallas kernels for 8% -> 9%
where the time goes in v3:
time: 122 us; the launch traced here: 121 us
  waiting for transfers between devices  49.3 us (40%)
  blocking collectives  29.8 us (24%)
  starting transfers between devices  21.4 us (18%)
  Pallas kernels  18.5 us (15%)
    ppermute x5, waiting for transfers between devices, swapped(): return lax.ppermute(x, axis, [(0, 1), (1, 0)])  28.6 us
    all_to_all x1, blocking collectives, on_device(): products = lax.all_to_all(products, 'ia', 0, 0, tiled=True)  19.1 us
    pallas_call x7, Pallas kernels, call(): pl.pallas_call(kernel, grid=grid, out_shape=out_shape, in_specs=in_specs,...  18.5 us
    all_to_all x1, blocking collectives, on_device(): pieces = lax.all_to_all(pieces, peers, 0, 0, tiled=True)  10.7 us
    all_to_all x1, waiting for transfers between devices, on_device(): sides = lax.all_to_all(sides, 'ia', 0, 0, tiled=True)  9.24 us
    all_to_all x1, starting transfers between devices, on_device(): grads = lax.all_to_all(grads, 'ia', 0, 0, tiled=True)  7.15 us
    all_to_all x1, waiting for transfers between devices, on_device(): pieces = lax.all_to_all(copies, everyone, 0, 0, tiled=True)  6.12 us
    ppermute x5, starting transfers between devices, swapped(): return lax.ppermute(x, axis, [(0, 1), (1, 0)])  5.67 us
  transfers between devices with their start and end apart: 8, of which 5 were waited for; matrix products, arithmetic and copies ran while one was open for 0% of the time, Pallas kernels for 9%

profile of v3, /device:TPU:0, one launch (start us, length us, event | category | flops | bytes accessed | tf_op | source)
XLA Modules:
  0.0 120.8 jit_solution(8077987257268366187)
XLA Ops:
  0.6 1.0 copy-done
  1.7 1.4 %shard_map.68 = bf16[64,32,128]{2,1,0:T(8,128)(2,1)} custom-call(bf16[32,64,128]{2,1,0:T(8,128)(2,1)S(1)} %copy-done), custom_call_target="tpu_custom_call" | custom-call | flops 1000000 | bytes 1048576 | tf_op jit(solution)/shard_map/pallas_call | solution.py:39
  3.1 7.1 %all-to-all-start = ((bf16[16,4,32,128]{3,2,1,0:T(8,128)(2,1)}), bf16[16,4,32,128]{3,2,1,0:T(8,128)(2,1)S(1)}, u32[]{:S(2)}, u32[]{:S(2)}) async-start(bf16[16,4,32,128]{3,2,1,0:T(8,128)(2,1)} %bitcast), calls=%async_computation | async-start | bytes 1048576 | tf_op jit(solution)/shard_map/all_to_all | solution.py:326
  10.2 6.2 %shard_map.69 = (bf16[16,2,4,32,128]{4,3,2,1,0:T(8,128)(2,1)}, bf16[16,256,256]{2,1,0:T(8,128)(2,1)}, bf16[16,128,256]{2,1,0:T(8,128)(2,1)}, f32[16,128,256]{2,1,0:T(8,128)}, f32[16,1,256]{2,1,0:T(1,128)}) custom-call(bf16[32,128,128]{2,1,0:T(8,128)(2,1)} %refs_0_.1, f32[1,128]{1,0:T(1,128)} %bitcast.12, bf16[256,128]{1,0:T(8,128)(2,1)} %bitcast.14, ...), custom_call_target="tpu_custom_call" | custom-call | flops 6000000000 | bytes 8388608 | tf_op jit(solution)/shard_map/pallas_call | solution.py:39
  16.4 5.4 %all-to-all-done.refs_1_ = bf16[16,4,32,128]{3,2,1,0:T(8,128)(2,1)S(1)} async-done(((bf16[16,4,32,128]{3,2,1,0:T(8,128)(2,1)}), bf16[16,4,32,128]{3,2,1,0:T(8,128)(2,1)S(1)}, u32[]{:S(2)}, u32[]{:S(2)}) %all-to-all-start) | async-done | bytes 524320 | tf_op jit(solution)/shard_map/all_to_all | solution.py:326
  21.8 1.9 %collective-permute-start.1 = (bf16[16,4,32,128]{3,2,1,0:T(8,128)(2,1)S(1)}, bf16[16,4,32,128]{3,2,1,0:T(8,128)(2,1)S(1)}, u32[]{:S(2)}, u32[]{:S(2)}) collective-permute-start(bf16[16,4,32,128]{3,2,1,0:T(8,128)(2,1)S(1)} %all-to-all-done.refs_1_), channel_id=1, source_target_pairs={{0,4},{4,0},{1,5},{5,1},{2,6},{6,2},{3,7},{7,3},{8,12},{12,8},{9,1... | collective-permute-start | bytes 1572872 | tf_op jit(solution)/shard_map/ppermute | solution.py:315
  23.7 3.7 %all-to-all-start.1 = ((bf16[16,2,4,32,128]{4,3,2,1,0:T(8,128)(2,1)}), bf16[16,2,4,32,128]{4,3,2,1,0:T(8,128)(2,1)S(1)}, u32[]{:S(2)}, u32[]{:S(2)}) async-start(bf16[16,2,4,32,128]{4,3,2,1,0:T(8,128)(2,1)} %get-tuple-element.14), calls=%async_computation.1 | async-start | bytes 2097152 | tf_op jit(solution)/shard_map/all_to_all | solution.py:330
  27.4 0.1 collective-permute-start
  27.5 6.8 %collective-permute-done.1.refs_3_ = bf16[16,4,32,128]{3,2,1,0:T(8,128)(2,1)S(1)} collective-permute-done((bf16[16,4,32,128]{3,2,1,0:T(8,128)(2,1)S(1)}, bf16[16,4,32,128]{3,2,1,0:T(8,128)(2,1)S(1)}, u32[]{:S(2)}, u32[]{:S(2)}) %collective-permute-start.1) | collective-permute-done | bytes 524320 | tf_op jit(solution)/shard_map/ppermute | solution.py:315
  34.2 0.0 collective-permute-start.2
  34.2 0.0 collective-permute-done.refs_2_
  34.2 9.2 %all-to-all-done.1.refs_0_ = bf16[16,2,4,32,128]{4,3,2,1,0:T(8,128)(2,1)S(1)} async-done(((bf16[16,2,4,32,128]{4,3,2,1,0:T(8,128)(2,1)}), bf16[16,2,4,32,128]{4,3,2,1,0:T(8,128)(2,1)S(1)}, u32[]{:S(2)}, u32[]{:S(2)}) %all-to-all-start.1) | async-done | bytes 1048608 | tf_op jit(solution)/shard_map/all_to_all | solution.py:330
  43.5 2.2 %shard_map.70 = bf16[16,2,4,32,128]{4,3,2,1,0:T(8,128)(2,1)S(1)} custom-call(bf16[16,2,4,32,128]{4,3,2,1,0:T(8,128)(2,1)S(1)} %all-to-all-done.1.refs_0_, bf16[16,4,32,128]{3,2,1,0:T(8,128)(2,1)S(1)} %all-to-all-done.refs_1_, bf16[16,4,32,128]{3,2,1,0:T(8,128)(2,1)S(1)} %collective-permute-done.refs_2_, ...), custom_call_target="tpu_custom_call" | custom-call | flops 4000000000 | bytes 5242880 | tf_op jit(solution)/shard_map/pallas_call | solution.py:39
  45.7 19.1 %all_to_all.25.refs_0_ = bf16[16,2,4,32,128]{4,3,2,1,0:T(8,128)(2,1)S(1)} all-to-all(bf16[16,2,4,32,128]{4,3,2,1,0:T(8,128)(2,1)S(1)} %shard_map.70), channel_id=1, replica_groups=mesh['ia'=16,'z_lo'=2,'core'=2,'col'=2] {'ia'}, dimensions={0} | all-to-all | bytes 2097152 | tf_op jit(solution)/shard_map/all_to_all | solution.py:334
  64.7 3.5 %shard_map.71 = (bf16[16,128,256]{2,1,0:T(8,128)(2,1)S(1)}, bf16[256,128]{1,0:T(8,128)(2,1)S(1)}) custom-call(bf16[16,2,4,32,128]{4,3,2,1,0:T(8,128)(2,1)S(1)} %all_to_all.25.refs_0_, bf16[16,256,256]{2,1,0:T(8,128)(2,1)} %get-tuple-element.16.refs_1_, bf16[16,128,256]{2,1,0:T(8,128)(2,1)} %get-tuple-element.17.refs_2_, bf16[256,128]{1,0:T(8,128)(2,1)} %bitcast.15), custom_call_target="tpu_custom_call" | custom-call | flops 6000000000 | bytes 8388608 | tf_op jit(solution)/shard_map/pallas_call | solution.py:39
  68.2 3.7 %collective-permute-start.4 = (bf16[16,128,256]{2,1,0:T(8,128)(2,1)S(1)}, bf16[16,128,256]{2,1,0:T(8,128)(2,1)S(1)}, u32[]{:S(2)}, u32[]{:S(2)}) collective-permute-start(bf16[16,128,256]{2,1,0:T(8,128)(2,1)S(1)} %get-tuple-element.21.own_ref), channel_id=1, source_target_pairs={{0,1},{1,0},{2,3},{3,2},{4,5},{5,4},{6,7},{7,6},{8,9},{9,8},{10,11... | collective-permute-start | bytes 3145736 | tf_op jit(solution)/shard_map/ppermute | solution.py:315
  71.9 21.8 %collective-permute-done.3 = bf16[256,128]{1,0:T(8,128)(2,1)S(1)} collective-permute-done((bf16[256,128]{1,0:T(8,128)(2,1)S(1)}, bf16[256,128]{1,0:T(8,128)(2,1)S(1)}, u32[]{:S(2)}, u32[]{:S(2)}) %collective-permute-start.3) | collective-permute-done | bytes 65568 | tf_op jit(solution)/shard_map/ppermute | solution.py:315
  93.7 10.7 %all_to_all.26.pieces_ref = f32[32,8,128]{2,1,0:T(8,128)S(1)} all-to-all(f32[32,8,128]{2,1,0:T(8,128)S(1)} %add_bitcast_fusion), channel_id=1, replica_groups=mesh['ia'=16,'z_lo'=2,'core'=2,'col'=2] {'ia','core'}, dimensions={0} | all-to-all | bytes 262144 | tf_op jit(solution)/shard_map/all_to_all | solution.py:340
  104.5 0.7 shard_map.72
  105.2 4.9 %all-to-all-start.4 = ((bf16[64,8,128]{2,1,0:T(8,128)(2,1)}), bf16[64,8,128]{2,1,0:T(8,128)(2,1)S(1)}, u32[]{:S(2)}, u32[]{:S(2)}) async-start(bf16[64,8,128]{2,1,0:T(8,128)(2,1)} %shard_map.72), calls=%async_computation.4 | async-start | bytes 262144 | tf_op jit(solution)/shard_map/all_to_all | solution.py:343
  110.1 0.0 collective-permute-done.4.other_ref
  110.1 3.8 %shard_map.73 = bf16[32,128,128]{2,1,0:T(8,128)(2,1)} custom-call(f32[16,128,256]{2,1,0:T(8,128)} %get-tuple-element.19.unit_ref, f32[16,1,256]{2,1,0:T(1,128)} %get-tuple-element.20.inv_ref, f32[1,128]{1,0:T(1,128)} %bitcast.13, bf16[16,128,256]{2,1,0:T(8,128)(2,1)S(1)} %get-tuple-element.21.own_ref, bf16[16,128,256]{2,1,0:T(8,128)(2,1)S(1)} %collective-permute-done.4.other_ref), custom_call_target="tpu_custom_call" | custom-call | flops 1000000000 | bytes 4194304 | tf_op jit(solution)/shard_map/pallas_call | solution.py:39
  113.8 6.1 %all-to-all-done.4.refs_0_ = bf16[64,8,128]{2,1,0:T(8,128)(2,1)S(1)} async-done(((bf16[64,8,128]{2,1,0:T(8,128)(2,1)}), bf16[64,8,128]{2,1,0:T(8,128)(2,1)S(1)}, u32[]{:S(2)}, u32[]{:S(2)}) %all-to-all-start.4) | async-done | bytes 131104 | tf_op jit(solution)/shard_map/all_to_all | solution.py:343
  119.9 0.8 shard_map.74
  (4 shorter events, 0.0 us)
Async XLA Ops:
  0.6 1.0 copy-start
  3.1 18.7 %all-to-all-start = ((bf16[16,4,32,128]{3,2,1,0:T(8,128)(2,1)}), bf16[16,4,32,128]{3,2,1,0:T(8,128)(2,1)S(1)}, u32[]{:S(2)}, u32[]{:S(2)}) async-start(bf16[16,4,32,128]{3,2,1,0:T(8,128)(2,1)} %bitcast), calls=%async_computation | async-start | bytes 1048576 | tf_op jit(solution)/shard_map/all_to_all | solution.py:326
  21.8 12.4 %collective-permute-start.1 = (bf16[16,4,32,128]{3,2,1,0:T(8,128)(2,1)S(1)}, bf16[16,4,32,128]{3,2,1,0:T(8,128)(2,1)S(1)}, u32[]{:S(2)}, u32[]{:S(2)}) collective-permute-start(bf16[16,4,32,128]{3,2,1,0:T(8,128)(2,1)S(1)} %all-to-all-done.refs_1_), channel_id=1, source_target_pairs={{0,4},{4,0},{1,5},{5,1},{2,6},{6,2},{3,7},{7,3},{8,12},{12,8},{9,1... | collective-permute-start | bytes 1572872 | tf_op jit(solution)/shard_map/ppermute | solution.py:315
  23.7 19.8 %all-to-all-start.1 = ((bf16[16,2,4,32,128]{4,3,2,1,0:T(8,128)(2,1)}), bf16[16,2,4,32,128]{4,3,2,1,0:T(8,128)(2,1)S(1)}, u32[]{:S(2)}, u32[]{:S(2)}) async-start(bf16[16,2,4,32,128]{4,3,2,1,0:T(8,128)(2,1)} %get-tuple-element.14), calls=%async_computation.1 | async-start | bytes 2097152 | tf_op jit(solution)/shard_map/all_to_all | solution.py:330
  27.4 6.9 %collective-permute-start = (bf16[16,4,32,128]{3,2,1,0:T(8,128)(2,1)S(1)}, bf16[16,4,32,128]{3,2,1,0:T(8,128)(2,1)S(1)}, u32[]{:S(2)}, u32[]{:S(2)}) collective-permute-start(bf16[16,4,32,128]{3,2,1,0:T(8,128)(2,1)S(1)} %all-to-all-done.refs_1_), channel_id=1, source_target_pairs={{0,2},{2,0},{1,3},{3,1},{4,6},{6,4},{5,7},{7,5},{8,10},{10,8},{9,1... | collective-permute-start | bytes 1572872 | tf_op jit(solution)/shard_map/ppermute | solution.py:315
  34.2 9.3 %collective-permute-start.2 = (bf16[16,4,32,128]{3,2,1,0:T(8,128)(2,1)S(1)}, bf16[16,4,32,128]{3,2,1,0:T(8,128)(2,1)S(1)}, u32[]{:S(2)}, u32[]{:S(2)}) collective-permute-start(bf16[16,4,32,128]{3,2,1,0:T(8,128)(2,1)S(1)} %collective-permute-done.1.refs_3_), channel_id=1, source_target_pairs={{0,2},{2,0},{1,3},{3,1},{4,6},{6,4},{5,7},{7,5},{8,10},{10,8},{9,1... | collective-permute-start | bytes 1572872 | tf_op jit(solution)/shard_map/ppermute | solution.py:315
  68.2 41.9 %collective-permute-start.4 = (bf16[16,128,256]{2,1,0:T(8,128)(2,1)S(1)}, bf16[16,128,256]{2,1,0:T(8,128)(2,1)S(1)}, u32[]{:S(2)}, u32[]{:S(2)}) collective-permute-start(bf16[16,128,256]{2,1,0:T(8,128)(2,1)S(1)} %get-tuple-element.21.own_ref), channel_id=1, source_target_pairs={{0,1},{1,0},{2,3},{3,2},{4,5},{5,4},{6,7},{7,6},{8,9},{9,8},{10,11... | collective-permute-start | bytes 3145736 | tf_op jit(solution)/shard_map/ppermute | solution.py:315
  71.9 21.8 %collective-permute-start.3 = (bf16[256,128]{1,0:T(8,128)(2,1)S(1)}, bf16[256,128]{1,0:T(8,128)(2,1)S(1)}, u32[]{:S(2)}, u32[]{:S(2)}) collective-permute-start(bf16[256,128]{1,0:T(8,128)(2,1)S(1)} %get-tuple-element.18), channel_id=1, source_target_pairs={{0,4},{4,0},{1,5},{5,1},{2,6},{6,2},{3,7},{7,3},{8,12},{12,8},{9,1... | collective-permute-start | bytes 196616 | tf_op jit(solution)/shard_map/ppermute | solution.py:315
  105.2 14.8 %all-to-all-start.4 = ((bf16[64,8,128]{2,1,0:T(8,128)(2,1)}), bf16[64,8,128]{2,1,0:T(8,128)(2,1)S(1)}, u32[]{:S(2)}, u32[]{:S(2)}) async-start(bf16[64,8,128]{2,1,0:T(8,128)(2,1)} %shard_map.72), calls=%async_computation.4 | async-start | bytes 262144 | tf_op jit(solution)/shard_map/all_to_all | solution.py:343

commit v4 on v3

--- a/solution.py
+++ b/solution.py
@@ -219,14 +219,14 @@
 
     @pl.when(step == pl.num_programs(0) - 1)
     def _():
-        raw_ref[...] = total[...].astype(BF)
+        raw_ref[...] = total[...]
 
 
 def gate(incoming, factors, normed, w, unroll=8, step=8):
     groups, _, per, rows, cols = incoming.shape
     return call(
         lambda *refs: gate_kernel(unroll, *refs),
-        [pltpu.VMEM(normed.shape, BF), pltpu.VMEM(w.shape, BF)],
+        [pltpu.VMEM(normed.shape, BF), pltpu.VMEM(w.shape, F32)],
         [kept(incoming), in_hbm(factors), in_hbm(normed), in_hbm(w)],
         [KEPT, leading(step, factors.shape), leading(step, normed.shape), fixed(w.shape)],
         [leading(step, normed.shape), fixed(w.shape)],
@@ -290,21 +290,28 @@
 def clip_kernel(axis, pieces_ref, out_ref):
     count, rows, depth = pieces_ref.shape
     here = lax.axis_index(axis)
+
+    def whole(group, core, col):
+        first = 8 * group + 2 * core + col
+        return pieces_ref[first].astype(F32) + pieces_ref[first + 4].astype(F32)
+
+    places = [(group, core) for group in range(count // 8) for core in range(2)]
     total = jnp.zeros((rows, depth), F32)
-    for n in range(count):
-        piece = pieces_ref[n].astype(F32)
-        total = total + piece * piece
+    for group, core in places:
+        for col in range(2):
+            piece = whole(group, core, col)
+            total = total + piece * piece
     squares = jnp.sum(jnp.sum(total, axis=0, keepdims=True), axis=1, keepdims=True)
     factor = jnp.minimum(1.0, CLIP_LIMIT * lax.rsqrt(squares + 1e-06))
-    for n in range(count // 2):
-        out_ref[n * rows : (n + 1) * rows, :] = pieces_ref[2 * n + here].astype(F32) * factor
+    for n, (group, core) in enumerate(places):
+        out_ref[n * rows : (n + 1) * rows, :] = whole(group, core, here) * factor
 
 
 def clip(pieces, axis="col"):
     count, rows, depth = pieces.shape
     return call(
         lambda *refs: clip_kernel(axis, *refs),
-        pltpu.HBM((count // 2 * rows, depth), F32),
+        pltpu.HBM((count // 4 * rows, depth), F32),
         [kept(pieces)],
         [KEPT],
         KEPT,
@@ -333,12 +340,11 @@
     products = triangle(sides, (grads, near, far, farther))
     products = lax.all_to_all(products, "ia", 0, 0, tiled=True)
     own, raw = gate(products, factors, normed, w)
-    raw = raw.astype(F32) + swapped(raw, "z_lo").astype(F32)
     other = swapped(own, "col")
     peers = ("ia", "core")
     pieces = raw.reshape(lax.axis_size(peers), -1, depth)
     pieces = lax.all_to_all(pieces, peers, 0, 0, tiled=True)
-    everyone = ("ia", "core", "col")
+    everyone = ("ia", "z_lo", "core", "col")
     copies = summed_copies(pieces, lax.axis_size(everyone))
     pieces = lax.all_to_all(copies, everyone, 0, 0, tiled=True)
     pair_grad = finish(unit, inv_std, norm_gain, own, other)

time: 122 us -> 101 us (0.83)
  waiting for transfers between devices: 49.3 us -> 28.1 us
    ppermute x5 -> x4, waiting for transfers between devices: 28.6 us -> 13.4 us  [swapped(): return lax.ppermute(x, axis, [(0, 1), (1, 0)])]
    all_to_all x1, waiting for transfers between devices: 6.12 us -> 0.12 us  [on_device(): pieces = lax.all_to_all(copies, everyone, 0, 0, tiled=True)]
    ppermute x5 -> x4, starting transfers between devices: 5.67 us -> 5.67 us  [swapped(): return lax.ppermute(x, axis, [(0, 1), (1, 0)])]
  transfers between devices with their start and end apart: 8 -> 7, of which waited for: 5 -> 5; matrix products, arithmetic and copies ran while one was open for 0% -> 0% of each run, Pallas kernels for 9% -> 11%
where the time goes in v4:
time: 101 us; the launch traced here: 99.4 us
  blocking collectives  30 us (30%)
  waiting for transfers between devices  28.1 us (28%)
  starting transfers between devices  21.1 us (21%)
  Pallas kernels  18.5 us (18%)
  local copies, waits for them, and re-layouts  1.03 us (1%)
    all_to_all x1, blocking collectives, on_device(): products = lax.all_to_all(products, 'ia', 0, 0, tiled=True)  19.1 us
    pallas_call x7, Pallas kernels, call(): pl.pallas_call(kernel, grid=grid, out_shape=out_shape, in_specs=in_specs,...  18.5 us
    ppermute x4, waiting for transfers between devices, swapped(): return lax.ppermute(x, axis, [(0, 1), (1, 0)])  13.4 us
    all_to_all x1, blocking collectives, on_device(): pieces = lax.all_to_all(pieces, peers, 0, 0, tiled=True)  10.9 us
    all_to_all x1, waiting for transfers between devices, on_device(): sides = lax.all_to_all(sides, 'ia', 0, 0, tiled=True)  9.24 us
    all_to_all x1, starting transfers between devices, on_device(): grads = lax.all_to_all(grads, 'ia', 0, 0, tiled=True)  7.15 us
    ppermute x4, starting transfers between devices, swapped(): return lax.ppermute(x, axis, [(0, 1), (1, 0)])  5.67 us
    all_to_all x1, waiting for transfers between devices, on_device(): grads = lax.all_to_all(grads, 'ia', 0, 0, tiled=True)  5.37 us
  transfers between devices with their start and end apart: 7, of which 5 were waited for; matrix products, arithmetic and copies ran while one was open for 0% of the time, Pallas kernels for 11%

profile of v4, /device:TPU:0, one launch (start us, length us, event | category | flops | bytes accessed | tf_op | source)
XLA Modules:
  0.0 99.4 jit_solution(11016090653564282566)
XLA Ops:
  0.6 1.0 %copy-done = bf16[32,64,128]{2,1,0:T(8,128)(2,1)S(1)} copy-done((bf16[32,64,128]{2,1,0:T(8,128)(2,1)S(1)}, bf16[32,64,128]{2,1,0:T(8,128)(2,1)}, u32[]{:S(2)}) %copy-start) | copy-done | bytes 524312
  1.7 1.4 %shard_map.68 = bf16[64,32,128]{2,1,0:T(8,128)(2,1)} custom-call(bf16[32,64,128]{2,1,0:T(8,128)(2,1)S(1)} %copy-done), custom_call_target="tpu_custom_call" | custom-call | flops 1000000 | bytes 1048576 | tf_op jit(solution)/shard_map/pallas_call | solution.py:39
  3.1 7.1 %all-to-all-start = ((bf16[16,4,32,128]{3,2,1,0:T(8,128)(2,1)}), bf16[16,4,32,128]{3,2,1,0:T(8,128)(2,1)S(1)}, u32[]{:S(2)}, u32[]{:S(2)}) async-start(bf16[16,4,32,128]{3,2,1,0:T(8,128)(2,1)} %bitcast), calls=%async_computation | async-start | bytes 1048576 | tf_op jit(solution)/shard_map/all_to_all | solution.py:333
  10.3 6.2 %shard_map.69 = (bf16[16,2,4,32,128]{4,3,2,1,0:T(8,128)(2,1)}, bf16[16,256,256]{2,1,0:T(8,128)(2,1)}, bf16[16,128,256]{2,1,0:T(8,128)(2,1)}, f32[16,128,256]{2,1,0:T(8,128)}, f32[16,1,256]{2,1,0:T(1,128)}) custom-call(bf16[32,128,128]{2,1,0:T(8,128)(2,1)} %refs_0_.1, f32[1,128]{1,0:T(1,128)} %bitcast.12, bf16[256,128]{1,0:T(8,128)(2,1)} %bitcast.14, ...), custom_call_target="tpu_custom_call" | custom-call | flops 6000000000 | bytes 8388608 | tf_op jit(solution)/shard_map/pallas_call | solution.py:39
  16.4 5.4 %all-to-all-done.refs_1_ = bf16[16,4,32,128]{3,2,1,0:T(8,128)(2,1)S(1)} async-done(((bf16[16,4,32,128]{3,2,1,0:T(8,128)(2,1)}), bf16[16,4,32,128]{3,2,1,0:T(8,128)(2,1)S(1)}, u32[]{:S(2)}, u32[]{:S(2)}) %all-to-all-start) | async-done | bytes 524320 | tf_op jit(solution)/shard_map/all_to_all | solution.py:333
  21.8 1.9 %collective-permute-start.1 = (bf16[16,4,32,128]{3,2,1,0:T(8,128)(2,1)S(1)}, bf16[16,4,32,128]{3,2,1,0:T(8,128)(2,1)S(1)}, u32[]{:S(2)}, u32[]{:S(2)}) collective-permute-start(bf16[16,4,32,128]{3,2,1,0:T(8,128)(2,1)S(1)} %all-to-all-done.refs_1_), channel_id=1, source_target_pairs={{0,4},{4,0},{1,5},{5,1},{2,6},{6,2},{3,7},{7,3},{8,12},{12,8},{9,1... | collective-permute-start | bytes 1572872 | tf_op jit(solution)/shard_map/ppermute | solution.py:322
  23.7 3.7 %all-to-all-start.1 = ((bf16[16,2,4,32,128]{4,3,2,1,0:T(8,128)(2,1)}), bf16[16,2,4,32,128]{4,3,2,1,0:T(8,128)(2,1)S(1)}, u32[]{:S(2)}, u32[]{:S(2)}) async-start(bf16[16,2,4,32,128]{4,3,2,1,0:T(8,128)(2,1)} %get-tuple-element.14), calls=%async_computation.1 | async-start | bytes 2097152 | tf_op jit(solution)/shard_map/all_to_all | solution.py:337
  27.4 0.1 collective-permute-start
  27.5 6.8 %collective-permute-done.1.refs_3_ = bf16[16,4,32,128]{3,2,1,0:T(8,128)(2,1)S(1)} collective-permute-done((bf16[16,4,32,128]{3,2,1,0:T(8,128)(2,1)S(1)}, bf16[16,4,32,128]{3,2,1,0:T(8,128)(2,1)S(1)}, u32[]{:S(2)}, u32[]{:S(2)}) %collective-permute-start.1) | collective-permute-done | bytes 524320 | tf_op jit(solution)/shard_map/ppermute | solution.py:322
  34.2 0.0 collective-permute-start.2
  34.2 0.0 collective-permute-done.refs_2_
  34.2 9.2 %all-to-all-done.1.refs_0_ = bf16[16,2,4,32,128]{4,3,2,1,0:T(8,128)(2,1)S(1)} async-done(((bf16[16,2,4,32,128]{4,3,2,1,0:T(8,128)(2,1)}), bf16[16,2,4,32,128]{4,3,2,1,0:T(8,128)(2,1)S(1)}, u32[]{:S(2)}, u32[]{:S(2)}) %all-to-all-start.1) | async-done | bytes 1048608 | tf_op jit(solution)/shard_map/all_to_all | solution.py:337
  43.5 0.0 collective-permute-done.2.refs_4_
  43.5 2.2 %shard_map.70 = bf16[16,2,4,32,128]{4,3,2,1,0:T(8,128)(2,1)S(1)} custom-call(bf16[16,2,4,32,128]{4,3,2,1,0:T(8,128)(2,1)S(1)} %all-to-all-done.1.refs_0_, bf16[16,4,32,128]{3,2,1,0:T(8,128)(2,1)S(1)} %all-to-all-done.refs_1_, bf16[16,4,32,128]{3,2,1,0:T(8,128)(2,1)S(1)} %collective-permute-done.refs_2_, ...), custom_call_target="tpu_custom_call" | custom-call | flops 4000000000 | bytes 5242880 | tf_op jit(solution)/shard_map/pallas_call | solution.py:39
  45.7 19.1 %all_to_all.25.refs_0_ = bf16[16,2,4,32,128]{4,3,2,1,0:T(8,128)(2,1)S(1)} all-to-all(bf16[16,2,4,32,128]{4,3,2,1,0:T(8,128)(2,1)S(1)} %shard_map.70), channel_id=1, replica_groups=mesh['ia'=16,'z_lo'=2,'core'=2,'col'=2] {'ia'}, dimensions={0} | all-to-all | bytes 2097152 | tf_op jit(solution)/shard_map/all_to_all | solution.py:341
  64.8 3.4 %shard_map.71 = (bf16[16,128,256]{2,1,0:T(8,128)(2,1)S(1)}, f32[256,128]{1,0:T(8,128)S(1)}) custom-call(bf16[16,2,4,32,128]{4,3,2,1,0:T(8,128)(2,1)S(1)} %all_to_all.25.refs_0_, bf16[16,256,256]{2,1,0:T(8,128)(2,1)} %get-tuple-element.16.refs_1_, bf16[16,128,256]{2,1,0:T(8,128)(2,1)} %get-tuple-element.17.refs_2_, bf16[256,128]{1,0:T(8,128)(2,1)} %bitcast.15), custom_call_target="tpu_custom_call" | custom-call | flops 6000000000 | bytes 8388608 | tf_op jit(solution)/shard_map/pallas_call | solution.py:39
  68.2 3.7 %collective-permute-start.3 = (bf16[16,128,256]{2,1,0:T(8,128)(2,1)S(1)}, bf16[16,128,256]{2,1,0:T(8,128)(2,1)S(1)}, u32[]{:S(2)}, u32[]{:S(2)}) collective-permute-start(bf16[16,128,256]{2,1,0:T(8,128)(2,1)S(1)} %get-tuple-element.21.own_ref), channel_id=1, source_target_pairs={{0,1},{1,0},{2,3},{3,2},{4,5},{5,4},{6,7},{7,6},{8,9},{9,8},{10,11... | collective-permute-start | bytes 3145736 | tf_op jit(solution)/shard_map/ppermute | solution.py:322
  71.9 10.9 %all_to_all.26.pieces_ref = f32[32,8,128]{2,1,0:T(8,128)S(1)} all-to-all(f32[32,8,128]{2,1,0:T(8,128)S(1)} %bitcast.10), channel_id=1, replica_groups=mesh['ia'=16,'z_lo'=2,'core'=2,'col'=2] {'ia','core'}, dimensions={0} | all-to-all | bytes 262144 | tf_op jit(solution)/shard_map/all_to_all | solution.py:346
  82.7 0.7 shard_map.72
  83.5 4.6 %all-to-all-start.4 = ((bf16[128,8,128]{2,1,0:T(8,128)(2,1)}), bf16[128,8,128]{2,1,0:T(8,128)(2,1)S(1)}, u32[]{:S(2)}, u32[]{:S(2)}) async-start(bf16[128,8,128]{2,1,0:T(8,128)(2,1)} %shard_map.72), calls=%async_computation.4 | async-start | bytes 524288 | tf_op jit(solution)/shard_map/all_to_all | solution.py:349
  88.1 6.6 %collective-permute-done.3.other_ref = bf16[16,128,256]{2,1,0:T(8,128)(2,1)S(1)} collective-permute-done((bf16[16,128,256]{2,1,0:T(8,128)(2,1)S(1)}, bf16[16,128,256]{2,1,0:T(8,128)(2,1)S(1)}, u32[]{:S(2)}, u32[]{:S(2)}) %collective-permute-start.3) | collective-permute-done | bytes 1048608 | tf_op jit(solution)/shard_map/ppermute | solution.py:322
  94.7 3.7 %shard_map.73 = bf16[32,128,128]{2,1,0:T(8,128)(2,1)} custom-call(f32[16,128,256]{2,1,0:T(8,128)} %get-tuple-element.19.unit_ref, f32[16,1,256]{2,1,0:T(1,128)} %get-tuple-element.20.inv_ref, f32[1,128]{1,0:T(1,128)} %bitcast.13, bf16[16,128,256]{2,1,0:T(8,128)(2,1)S(1)} %get-tuple-element.21.own_ref, bf16[16,128,256]{2,1,0:T(8,128)(2,1)S(1)} %collective-permute-done.3.other_ref), custom_call_target="tpu_custom_call" | custom-call | flops 1000000000 | bytes 4194304 | tf_op jit(solution)/shard_map/pallas_call | solution.py:39
  98.5 0.1 all-to-all-done.4.refs_0_
  98.6 0.8 shard_map.74
  (1 shorter events, 0.0 us)
Async XLA Ops:
  0.6 1.0 %copy-start = (bf16[32,64,128]{2,1,0:T(8,128)(2,1)S(1)}, bf16[32,64,128]{2,1,0:T(8,128)(2,1)}, u32[]{:S(2)}) copy-start(bf16[32,64,128]{2,1,0:T(8,128)(2,1)} %x_ref.1) | copy-start | bytes 1572868
  3.1 18.7 %all-to-all-start = ((bf16[16,4,32,128]{3,2,1,0:T(8,128)(2,1)}), bf16[16,4,32,128]{3,2,1,0:T(8,128)(2,1)S(1)}, u32[]{:S(2)}, u32[]{:S(2)}) async-start(bf16[16,4,32,128]{3,2,1,0:T(8,128)(2,1)} %bitcast), calls=%async_computation | async-start | bytes 1048576 | tf_op jit(solution)/shard_map/all_to_all | solution.py:333
  21.8 12.4 %collective-permute-start.1 = (bf16[16,4,32,128]{3,2,1,0:T(8,128)(2,1)S(1)}, bf16[16,4,32,128]{3,2,1,0:T(8,128)(2,1)S(1)}, u32[]{:S(2)}, u32[]{:S(2)}) collective-permute-start(bf16[16,4,32,128]{3,2,1,0:T(8,128)(2,1)S(1)} %all-to-all-done.refs_1_), channel_id=1, source_target_pairs={{0,4},{4,0},{1,5},{5,1},{2,6},{6,2},{3,7},{7,3},{8,12},{12,8},{9,1... | collective-permute-start | bytes 1572872 | tf_op jit(solution)/shard_map/ppermute | solution.py:322
  23.7 19.8 %all-to-all-start.1 = ((bf16[16,2,4,32,128]{4,3,2,1,0:T(8,128)(2,1)}), bf16[16,2,4,32,128]{4,3,2,1,0:T(8,128)(2,1)S(1)}, u32[]{:S(2)}, u32[]{:S(2)}) async-start(bf16[16,2,4,32,128]{4,3,2,1,0:T(8,128)(2,1)} %get-tuple-element.14), calls=%async_computation.1 | async-start | bytes 2097152 | tf_op jit(solution)/shard_map/all_to_all | solution.py:337
  27.4 6.9 %collective-permute-start = (bf16[16,4,32,128]{3,2,1,0:T(8,128)(2,1)S(1)}, bf16[16,4,32,128]{3,2,1,0:T(8,128)(2,1)S(1)}, u32[]{:S(2)}, u32[]{:S(2)}) collective-permute-start(bf16[16,4,32,128]{3,2,1,0:T(8,128)(2,1)S(1)} %all-to-all-done.refs_1_), channel_id=1, source_target_pairs={{0,2},{2,0},{1,3},{3,1},{4,6},{6,4},{5,7},{7,5},{8,10},{10,8},{9,1... | collective-permute-start | bytes 1572872 | tf_op jit(solution)/shard_map/ppermute | solution.py:322
  34.2 9.3 %collective-permute-start.2 = (bf16[16,4,32,128]{3,2,1,0:T(8,128)(2,1)S(1)}, bf16[16,4,32,128]{3,2,1,0:T(8,128)(2,1)S(1)}, u32[]{:S(2)}, u32[]{:S(2)}) collective-permute-start(bf16[16,4,32,128]{3,2,1,0:T(8,128)(2,1)S(1)} %collective-permute-done.1.refs_3_), channel_id=1, source_target_pairs={{0,2},{2,0},{1,3},{3,1},{4,6},{6,4},{5,7},{7,5},{8,10},{10,8},{9,1... | collective-permute-start | bytes 1572872 | tf_op jit(solution)/shard_map/ppermute | solution.py:322
  68.2 26.5 %collective-permute-start.3 = (bf16[16,128,256]{2,1,0:T(8,128)(2,1)S(1)}, bf16[16,128,256]{2,1,0:T(8,128)(2,1)S(1)}, u32[]{:S(2)}, u32[]{:S(2)}) collective-permute-start(bf16[16,128,256]{2,1,0:T(8,128)(2,1)S(1)} %get-tuple-element.21.own_ref), channel_id=1, source_target_pairs={{0,1},{1,0},{2,3},{3,2},{4,5},{5,4},{6,7},{7,6},{8,9},{9,8},{10,11... | collective-permute-start | bytes 3145736 | tf_op jit(solution)/shard_map/ppermute | solution.py:322
  83.5 15.1 %all-to-all-start.4 = ((bf16[128,8,128]{2,1,0:T(8,128)(2,1)}), bf16[128,8,128]{2,1,0:T(8,128)(2,1)S(1)}, u32[]{:S(2)}, u32[]{:S(2)}) async-start(bf16[128,8,128]{2,1,0:T(8,128)(2,1)} %shard_map.72), calls=%async_computation.4 | async-start | bytes 524288 | tf_op jit(solution)/shard_map/all_to_all | solution.py:349

commit v5 on v4

--- a/solution.py
+++ b/solution.py
@@ -97,7 +97,7 @@
         inv_std = lax.rsqrt(jnp.mean(centred * centred, axis=0, keepdims=True) + 1e-05)
         unit = centred * inv_std
         normed = (unit * gains[...]).astype(BF)
-        unit_ref[p] = unit
+        unit_ref[p] = unit.astype(BF)
         inv_ref[p] = inv_std
         normed_ref[p] = normed
         proj = dot(w, normed)
@@ -132,7 +132,7 @@
         pltpu.HBM((groups, 2, per, rows, cols), BF),
         pltpu.HBM((pairs, 4 * half, 2 * cols), BF),
         pltpu.HBM((pairs, depth, 2 * cols), BF),
-        pltpu.HBM((pairs, depth, 2 * cols), F32),
+        pltpu.HBM((pairs, depth, 2 * cols), BF),
         pltpu.HBM((pairs, 1, 2 * cols), F32),
     ]
     table = mask.reshape(-1, cols)
@@ -237,6 +237,15 @@
     )
 
 
+def fetch_kernel(x_ref, out_ref):
+    out_ref[...] = x_ref[...]
+
+
+def fetch(x, step=8):
+    spec = leading(step, x.shape)
+    return call(fetch_kernel, pltpu.VMEM(x.shape, x.dtype), [in_hbm(x)], [spec], spec, grid=(x.shape[0] // step,), flops=10**9)
+
+
 def finish_kernel(unit_ref, inv_ref, gain_ref, own_ref, other_ref, out_ref, gains):
     step, cols, depth = out_ref.shape
 
@@ -247,7 +256,7 @@
     turn = identity(2 * cols).astype(BF)
     base = pl.program_id(0) * (step // 2)
     for q in range(step // 2):
-        unit = unit_ref[q]
+        unit = unit_ref[q].astype(F32)
         scaled = (own_ref[base + q].astype(F32) + other_ref[base + q].astype(F32)) * gains[...]
         mean = jnp.mean(scaled, axis=0, keepdims=True)
         along = jnp.mean(scaled * unit, axis=0, keepdims=True)
@@ -262,7 +271,7 @@
     return call(
         finish_kernel,
         jax.ShapeDtypeStruct(shape, BF),
-        [in_hbm(unit), in_hbm(inv_std), in_hbm(gain[None]), kept(own), kept(other)],
+        [kept(unit), in_hbm(inv_std), in_hbm(gain[None]), kept(own), kept(other)],
         [leading(half, unit.shape), leading(half, inv_std.shape), fixed((1, depth)), KEPT, KEPT],
         leading(step, shape),
         [pltpu.VMEM((depth, twice), F32)],
@@ -310,11 +319,7 @@
 def clip(pieces, axis="col"):
     count, rows, depth = pieces.shape
     return call(
-        lambda *refs: clip_kernel(axis, *refs),
-        pltpu.HBM((count // 4 * rows, depth), F32),
-        [kept(pieces)],
-        [KEPT],
-        KEPT,
+        lambda *refs: clip_kernel(axis, *refs), pltpu.HBM((count // 4 * rows, depth), F32), [kept(pieces)], [KEPT], KEPT
     )
 
 
@@ -346,7 +351,9 @@
     pieces = lax.all_to_all(pieces, peers, 0, 0, tiled=True)
     everyone = ("ia", "z_lo", "core", "col")
     copies = summed_copies(pieces, lax.axis_size(everyone))
+    unit, copies = lax.optimization_barrier((unit, copies))
     pieces = lax.all_to_all(copies, everyone, 0, 0, tiled=True)
+    unit = fetch(unit)
     pair_grad = finish(unit, inv_std, norm_gain, own, other)
     pieces, pair_grad = lax.optimization_barrier((pieces, pair_grad))
     weight_grads = jnp.swapaxes(clip(pieces).reshape(4, chans, depth), 1, 2)

time: 101 us -> 101 us (level)
    ppermute x4, waiting for transfers between devices: 13.4 us -> 12.2 us  [swapped(): return lax.ppermute(x, axis, [(0, 1), (1, 0)])]
    pallas_call x7 -> x8, Pallas kernels: 18.5 us -> 19.4 us  [call(): pl.pallas_call(kernel, grid=grid, out_shape=out_shape, in_specs=in_specs,...]
  transfers between devices with their start and end apart: 7 -> 7, of which waited for: 5 -> 5; matrix products, arithmetic and copies ran while one was open for 0% -> 0% of each run, Pallas kernels for 11% -> 12%
where the time goes in v5:
time: 101 us; the launch traced here: 99.4 us
  blocking collectives  30 us (30%)
  waiting for transfers between devices  27.2 us (27%)
  starting transfers between devices  21 us (21%)
  Pallas kernels  19.4 us (19%)
  local copies, waits for them, and re-layouts  1.03 us (1%)
    pallas_call x8, Pallas kernels, call(): pl.pallas_call(kernel, grid=grid, out_shape=out_shape, in_specs=in_specs,...  19.4 us
    all_to_all x1, blocking collectives, on_device(): products = lax.all_to_all(products, 'ia', 0, 0, tiled=True)  19.1 us
    ppermute x4, waiting for transfers between devices, swapped(): return lax.ppermute(x, axis, [(0, 1), (1, 0)])  12.2 us
    all_to_all x1, blocking collectives, on_device(): pieces = lax.all_to_all(pieces, peers, 0, 0, tiled=True)  10.9 us
    all_to_all x1, waiting for transfers between devices, on_device(): sides = lax.all_to_all(sides, 'ia', 0, 0, tiled=True)  9.24 us
    all_to_all x1, starting transfers between devices, on_device(): grads = lax.all_to_all(grads, 'ia', 0, 0, tiled=True)  7.15 us
    ppermute x4, starting transfers between devices, swapped(): return lax.ppermute(x, axis, [(0, 1), (1, 0)])  5.66 us
    all_to_all x1, waiting for transfers between devices, on_device(): grads = lax.all_to_all(grads, 'ia', 0, 0, tiled=True)  5.34 us
  transfers between devices with their start and end apart: 7, of which 5 were waited for; matrix products, arithmetic and copies ran while one was open for 0% of the time, Pallas kernels for 12%

profile of v5, /device:TPU:0, one launch (start us, length us, event | category | flops | bytes accessed | tf_op | source)
XLA Modules:
  0.0 99.4 jit_solution(8488563523460897926)
XLA Ops:
  0.6 1.0 %copy-done = bf16[32,64,128]{2,1,0:T(8,128)(2,1)S(1)} copy-done((bf16[32,64,128]{2,1,0:T(8,128)(2,1)S(1)}, bf16[32,64,128]{2,1,0:T(8,128)(2,1)}, u32[]{:S(2)}) %copy-start) | copy-done | bytes 524312
  1.7 1.4 %shard_map.69 = bf16[64,32,128]{2,1,0:T(8,128)(2,1)} custom-call(bf16[32,64,128]{2,1,0:T(8,128)(2,1)S(1)} %copy-done), custom_call_target="tpu_custom_call" | custom-call | flops 1000000 | bytes 1048576 | tf_op jit(solution)/shard_map/pallas_call | solution.py:39
  3.1 7.1 %all-to-all-start = ((bf16[16,4,32,128]{3,2,1,0:T(8,128)(2,1)}), bf16[16,4,32,128]{3,2,1,0:T(8,128)(2,1)S(1)}, u32[]{:S(2)}, u32[]{:S(2)}) async-start(bf16[16,4,32,128]{3,2,1,0:T(8,128)(2,1)} %bitcast.4), calls=%async_computation | async-start | bytes 1048576 | tf_op jit(solution)/shard_map/all_to_all | solution.py:338
  10.2 6.2 %shard_map.68 = (bf16[16,2,4,32,128]{4,3,2,1,0:T(8,128)(2,1)}, bf16[16,256,256]{2,1,0:T(8,128)(2,1)}, bf16[16,128,256]{2,1,0:T(8,128)(2,1)}, bf16[16,128,256]{2,1,0:T(8,128)(2,1)}, f32[16,1,256]{2,1,0:T(1,128)}) custom-call(bf16[32,128,128]{2,1,0:T(8,128)(2,1)} %refs_0_.1, f32[1,128]{1,0:T(1,128)} %bitcast.12, bf16[256,128]{1,0:T(8,128)(2,1)} %bitcast.14, ...), custom_call_target="tpu_custom_call" | custom-call | flops 6000000000 | bytes 8388608 | tf_op jit(solution)/shard_map/pallas_call | solution.py:39
  16.4 5.3 %all-to-all-done.refs_1_ = bf16[16,4,32,128]{3,2,1,0:T(8,128)(2,1)S(1)} async-done(((bf16[16,4,32,128]{3,2,1,0:T(8,128)(2,1)}), bf16[16,4,32,128]{3,2,1,0:T(8,128)(2,1)S(1)}, u32[]{:S(2)}, u32[]{:S(2)}) %all-to-all-start) | async-done | bytes 524320 | tf_op jit(solution)/shard_map/all_to_all | solution.py:338
  21.7 1.9 %collective-permute-start.1 = (bf16[16,4,32,128]{3,2,1,0:T(8,128)(2,1)S(1)}, bf16[16,4,32,128]{3,2,1,0:T(8,128)(2,1)S(1)}, u32[]{:S(2)}, u32[]{:S(2)}) collective-permute-start(bf16[16,4,32,128]{3,2,1,0:T(8,128)(2,1)S(1)} %all-to-all-done.refs_1_), channel_id=1, source_target_pairs={{0,4},{4,0},{1,5},{5,1},{2,6},{6,2},{3,7},{7,3},{8,12},{12,8},{9,1... | collective-permute-start | bytes 1572872 | tf_op jit(solution)/shard_map/ppermute | solution.py:327
  23.7 3.7 %all-to-all-start.1 = ((bf16[16,2,4,32,128]{4,3,2,1,0:T(8,128)(2,1)}), bf16[16,2,4,32,128]{4,3,2,1,0:T(8,128)(2,1)S(1)}, u32[]{:S(2)}, u32[]{:S(2)}) async-start(bf16[16,2,4,32,128]{4,3,2,1,0:T(8,128)(2,1)} %get-tuple-element.17), calls=%async_computation.1 | async-start | bytes 2097152 | tf_op jit(solution)/shard_map/all_to_all | solution.py:342
  27.3 0.1 collective-permute-start
  27.4 6.8 %collective-permute-done.1.refs_3_ = bf16[16,4,32,128]{3,2,1,0:T(8,128)(2,1)S(1)} collective-permute-done((bf16[16,4,32,128]{3,2,1,0:T(8,128)(2,1)S(1)}, bf16[16,4,32,128]{3,2,1,0:T(8,128)(2,1)S(1)}, u32[]{:S(2)}, u32[]{:S(2)}) %collective-permute-start.1) | collective-permute-done | bytes 524320 | tf_op jit(solution)/shard_map/ppermute | solution.py:327
  34.2 0.0 collective-permute-start.2
  34.2 9.2 %all-to-all-done.1.refs_0_ = bf16[16,2,4,32,128]{4,3,2,1,0:T(8,128)(2,1)S(1)} async-done(((bf16[16,2,4,32,128]{4,3,2,1,0:T(8,128)(2,1)}), bf16[16,2,4,32,128]{4,3,2,1,0:T(8,128)(2,1)S(1)}, u32[]{:S(2)}, u32[]{:S(2)}) %all-to-all-start.1) | async-done | bytes 1048608 | tf_op jit(solution)/shard_map/all_to_all | solution.py:342
  43.4 0.0 collective-permute-done.2.refs_4_
  43.4 2.2 %shard_map.70 = bf16[16,2,4,32,128]{4,3,2,1,0:T(8,128)(2,1)S(1)} custom-call(bf16[16,2,4,32,128]{4,3,2,1,0:T(8,128)(2,1)S(1)} %all-to-all-done.1.refs_0_, bf16[16,4,32,128]{3,2,1,0:T(8,128)(2,1)S(1)} %all-to-all-done.refs_1_, bf16[16,4,32,128]{3,2,1,0:T(8,128)(2,1)S(1)} %collective-permute-done.refs_2_, ...), custom_call_target="tpu_custom_call" | custom-call | flops 4000000000 | bytes 5242880 | tf_op jit(solution)/shard_map/pallas_call | solution.py:39
  45.6 19.1 %all_to_all.25.refs_0_ = bf16[16,2,4,32,128]{4,3,2,1,0:T(8,128)(2,1)S(1)} all-to-all(bf16[16,2,4,32,128]{4,3,2,1,0:T(8,128)(2,1)S(1)} %shard_map.70), channel_id=1, replica_groups=mesh['ia'=16,'z_lo'=2,'core'=2,'col'=2] {'ia'}, dimensions={0} | all-to-all | bytes 2097152 | tf_op jit(solution)/shard_map/all_to_all | solution.py:346
  64.7 3.5 %shard_map.71 = (bf16[16,128,256]{2,1,0:T(8,128)(2,1)S(1)}, f32[256,128]{1,0:T(8,128)S(1)}) custom-call(bf16[16,2,4,32,128]{4,3,2,1,0:T(8,128)(2,1)S(1)} %all_to_all.25.refs_0_, bf16[16,256,256]{2,1,0:T(8,128)(2,1)} %get-tuple-element.19.refs_1_, bf16[16,128,256]{2,1,0:T(8,128)(2,1)} %get-tuple-element.20.refs_2_, bf16[256,128]{1,0:T(8,128)(2,1)} %bitcast.15), custom_call_target="tpu_custom_call" | custom-call | flops 6000000000 | bytes 8388608 | tf_op jit(solution)/shard_map/pallas_call | solution.py:39
  68.2 3.7 %collective-permute-start.3 = (bf16[16,128,256]{2,1,0:T(8,128)(2,1)S(1)}, bf16[16,128,256]{2,1,0:T(8,128)(2,1)S(1)}, u32[]{:S(2)}, u32[]{:S(2)}) collective-permute-start(bf16[16,128,256]{2,1,0:T(8,128)(2,1)S(1)} %get-tuple-element.25.own_ref), channel_id=1, source_target_pairs={{0,1},{1,0},{2,3},{3,2},{4,5},{5,4},{6,7},{7,6},{8,9},{9,8},{10,11... | collective-permute-start | bytes 3145736 | tf_op jit(solution)/shard_map/ppermute | solution.py:327
  71.8 10.9 %all_to_all.26.pieces_ref = f32[32,8,128]{2,1,0:T(8,128)S(1)} all-to-all(f32[32,8,128]{2,1,0:T(8,128)S(1)} %bitcast.10), channel_id=1, replica_groups=mesh['ia'=16,'z_lo'=2,'core'=2,'col'=2] {'ia','core'}, dimensions={0} | all-to-all | bytes 262144 | tf_op jit(solution)/shard_map/all_to_all | solution.py:351
  82.7 0.8 shard_map.72
  83.4 4.6 %all-to-all-start.4 = ((bf16[128,8,128]{2,1,0:T(8,128)(2,1)}), bf16[128,8,128]{2,1,0:T(8,128)(2,1)S(1)}, u32[]{:S(2)}, u32[]{:S(2)}) async-start(bf16[128,8,128]{2,1,0:T(8,128)(2,1)} %shard_map.72), calls=%async_computation.4 | async-start | bytes 524288 | tf_op jit(solution)/shard_map/all_to_all | solution.py:355
  88.0 1.3 %shard_map.73.unit_ref = bf16[16,128,256]{2,1,0:T(8,128)(2,1)S(1)} custom-call(bf16[16,128,256]{2,1,0:T(8,128)(2,1)} %get-tuple-element.23.x_ref), custom_call_target="tpu_custom_call" | custom-call | flops 1000000000 | bytes 1048576 | tf_op jit(solution)/shard_map/pallas_call | solution.py:39
  89.3 5.4 %collective-permute-done.3.other_ref = bf16[16,128,256]{2,1,0:T(8,128)(2,1)S(1)} collective-permute-done((bf16[16,128,256]{2,1,0:T(8,128)(2,1)S(1)}, bf16[16,128,256]{2,1,0:T(8,128)(2,1)S(1)}, u32[]{:S(2)}, u32[]{:S(2)}) %collective-permute-start.3) | collective-permute-done | bytes 1048608 | tf_op jit(solution)/shard_map/ppermute | solution.py:327
  94.7 3.3 %shard_map.74 = bf16[32,128,128]{2,1,0:T(8,128)(2,1)} custom-call(bf16[16,128,256]{2,1,0:T(8,128)(2,1)S(1)} %shard_map.73.unit_ref, f32[16,1,256]{2,1,0:T(1,128)} %get-tuple-element.24.inv_ref, f32[1,128]{1,0:T(1,128)} %bitcast.13, bf16[16,128,256]{2,1,0:T(8,128)(2,1)S(1)} %get-tuple-element.25.own_ref, ...), custom_call_target="tpu_custom_call" | custom-call | flops 1000000000 | bytes 4194304 | tf_op jit(solution)/shard_map/pallas_call | solution.py:39
  98.0 0.5 all-to-all-done.4.refs_0_
  98.5 0.8 shard_map.75
  (2 shorter events, 0.0 us)
Async XLA Ops:
  0.6 1.0 %copy-start = (bf16[32,64,128]{2,1,0:T(8,128)(2,1)S(1)}, bf16[32,64,128]{2,1,0:T(8,128)(2,1)}, u32[]{:S(2)}) copy-start(bf16[32,64,128]{2,1,0:T(8,128)(2,1)} %x_ref.1) | copy-start | bytes 1572868
  3.1 18.7 %all-to-all-start = ((bf16[16,4,32,128]{3,2,1,0:T(8,128)(2,1)}), bf16[16,4,32,128]{3,2,1,0:T(8,128)(2,1)S(1)}, u32[]{:S(2)}, u32[]{:S(2)}) async-start(bf16[16,4,32,128]{3,2,1,0:T(8,128)(2,1)} %bitcast.4), calls=%async_computation | async-start | bytes 1048576 | tf_op jit(solution)/shard_map/all_to_all | solution.py:338
  21.7 12.4 %collective-permute-start.1 = (bf16[16,4,32,128]{3,2,1,0:T(8,128)(2,1)S(1)}, bf16[16,4,32,128]{3,2,1,0:T(8,128)(2,1)S(1)}, u32[]{:S(2)}, u32[]{:S(2)}) collective-permute-start(bf16[16,4,32,128]{3,2,1,0:T(8,128)(2,1)S(1)} %all-to-all-done.refs_1_), channel_id=1, source_target_pairs={{0,4},{4,0},{1,5},{5,1},{2,6},{6,2},{3,7},{7,3},{8,12},{12,8},{9,1... | collective-permute-start | bytes 1572872 | tf_op jit(solution)/shard_map/ppermute | solution.py:327
  23.7 19.8 %all-to-all-start.1 = ((bf16[16,2,4,32,128]{4,3,2,1,0:T(8,128)(2,1)}), bf16[16,2,4,32,128]{4,3,2,1,0:T(8,128)(2,1)S(1)}, u32[]{:S(2)}, u32[]{:S(2)}) async-start(bf16[16,2,4,32,128]{4,3,2,1,0:T(8,128)(2,1)} %get-tuple-element.17), calls=%async_computation.1 | async-start | bytes 2097152 | tf_op jit(solution)/shard_map/all_to_all | solution.py:342
  27.3 6.9 %collective-permute-start = (bf16[16,4,32,128]{3,2,1,0:T(8,128)(2,1)S(1)}, bf16[16,4,32,128]{3,2,1,0:T(8,128)(2,1)S(1)}, u32[]{:S(2)}, u32[]{:S(2)}) collective-permute-start(bf16[16,4,32,128]{3,2,1,0:T(8,128)(2,1)S(1)} %all-to-all-done.refs_1_), channel_id=1, source_target_pairs={{0,2},{2,0},{1,3},{3,1},{4,6},{6,4},{5,7},{7,5},{8,10},{10,8},{9,1... | collective-permute-start | bytes 1572872 | tf_op jit(solution)/shard_map/ppermute | solution.py:327
  34.2 9.3 %collective-permute-start.2 = (bf16[16,4,32,128]{3,2,1,0:T(8,128)(2,1)S(1)}, bf16[16,4,32,128]{3,2,1,0:T(8,128)(2,1)S(1)}, u32[]{:S(2)}, u32[]{:S(2)}) collective-permute-start(bf16[16,4,32,128]{3,2,1,0:T(8,128)(2,1)S(1)} %collective-permute-done.1.refs_3_), channel_id=1, source_target_pairs={{0,2},{2,0},{1,3},{3,1},{4,6},{6,4},{5,7},{7,5},{8,10},{10,8},{9,1... | collective-permute-start | bytes 1572872 | tf_op jit(solution)/shard_map/ppermute | solution.py:327
  68.2 26.5 %collective-permute-start.3 = (bf16[16,128,256]{2,1,0:T(8,128)(2,1)S(1)}, bf16[16,128,256]{2,1,0:T(8,128)(2,1)S(1)}, u32[]{:S(2)}, u32[]{:S(2)}) collective-permute-start(bf16[16,128,256]{2,1,0:T(8,128)(2,1)S(1)} %get-tuple-element.25.own_ref), channel_id=1, source_target_pairs={{0,1},{1,0},{2,3},{3,2},{4,5},{5,4},{6,7},{7,6},{8,9},{9,8},{10,11... | collective-permute-start | bytes 3145736 | tf_op jit(solution)/shard_map/ppermute | solution.py:327
  83.4 15.1 %all-to-all-start.4 = ((bf16[128,8,128]{2,1,0:T(8,128)(2,1)}), bf16[128,8,128]{2,1,0:T(8,128)(2,1)S(1)}, u32[]{:S(2)}, u32[]{:S(2)}) async-start(bf16[128,8,128]{2,1,0:T(8,128)(2,1)} %shard_map.72), calls=%async_computation.4 | async-start | bytes 524288 | tf_op jit(solution)/shard_map/all_to_all | solution.py:355

commit v6 on v5

--- a/solution.py
+++ b/solution.py
@@ -219,14 +219,14 @@
 
     @pl.when(step == pl.num_programs(0) - 1)
     def _():
-        raw_ref[...] = total[...]
+        raw_ref[...] = total[...].astype(BF)
 
 
 def gate(incoming, factors, normed, w, unroll=8, step=8):
     groups, _, per, rows, cols = incoming.shape
     return call(
         lambda *refs: gate_kernel(unroll, *refs),
-        [pltpu.VMEM(normed.shape, BF), pltpu.VMEM(w.shape, F32)],
+        [pltpu.VMEM(normed.shape, BF), pltpu.VMEM(w.shape, BF)],
         [kept(incoming), in_hbm(factors), in_hbm(normed), in_hbm(w)],
         [KEPT, leading(step, factors.shape), leading(step, normed.shape), fixed(w.shape)],
         [leading(step, normed.shape), fixed(w.shape)],
@@ -283,9 +283,9 @@
 
 def gather_kernel(pieces_ref, out_ref):
     count, _, _ = pieces_ref.shape
-    total = pieces_ref[0]
+    total = pieces_ref[0].astype(F32)
     for n in range(1, count):
-        total = total + pieces_ref[n]
+        total = total + pieces_ref[n].astype(F32)
     piece = total.astype(BF)
     for n in range(out_ref.shape[0]):
         out_ref[n] = piece

time: 101 us -> 100 us (0.990)
  no operation moved by 1% of the time
where the time goes in v6:
time: 100 us; the launch traced here: 99.1 us
  blocking collectives  29.7 us (30%)
  waiting for transfers between devices  27.2 us (27%)
  starting transfers between devices  21 us (21%)
  Pallas kernels  19.4 us (19%)
  local copies, waits for them, and re-layouts  1.03 us (1%)
    pallas_call x8, Pallas kernels, call(): pl.pallas_call(kernel, grid=grid, out_shape=out_shape, in_specs=in_specs,...  19.4 us
    all_to_all x1, blocking collectives, on_device(): products = lax.all_to_all(products, 'ia', 0, 0, tiled=True)  19.1 us
    ppermute x4, waiting for transfers between devices, swapped(): return lax.ppermute(x, axis, [(0, 1), (1, 0)])  12.5 us
    all_to_all x1, blocking collectives, on_device(): pieces = lax.all_to_all(pieces, peers, 0, 0, tiled=True)  10.6 us
    all_to_all x1, waiting for transfers between devices, on_device(): sides = lax.all_to_all(sides, 'ia', 0, 0, tiled=True)  9.24 us
    all_to_all x1, starting transfers between devices, on_device(): grads = lax.all_to_all(grads, 'ia', 0, 0, tiled=True)  7.15 us
    ppermute x4, starting transfers between devices, swapped(): return lax.ppermute(x, axis, [(0, 1), (1, 0)])  5.66 us
    all_to_all x1, waiting for transfers between devices, on_device(): grads = lax.all_to_all(grads, 'ia', 0, 0, tiled=True)  5.34 us
  transfers between devices with their start and end apart: 7, of which 5 were waited for; matrix products, arithmetic and copies ran while one was open for 0% of the time, Pallas kernels for 12%

profile of v6, /device:TPU:0, one launch (start us, length us, event | category | flops | bytes accessed | tf_op | source)
XLA Modules:
  0.0 99.1 jit_solution(5011650617326476582)
XLA Ops:
  0.6 1.0 %copy-done = bf16[32,64,128]{2,1,0:T(8,128)(2,1)S(1)} copy-done((bf16[32,64,128]{2,1,0:T(8,128)(2,1)S(1)}, bf16[32,64,128]{2,1,0:T(8,128)(2,1)}, u32[]{:S(2)}) %copy-start) | copy-done | bytes 524312
  1.7 1.4 %shard_map.69 = bf16[64,32,128]{2,1,0:T(8,128)(2,1)} custom-call(bf16[32,64,128]{2,1,0:T(8,128)(2,1)S(1)} %copy-done), custom_call_target="tpu_custom_call" | custom-call | flops 1000000 | bytes 1048576 | tf_op jit(solution)/shard_map/pallas_call | solution.py:39
  3.1 7.1 %all-to-all-start = ((bf16[16,4,32,128]{3,2,1,0:T(8,128)(2,1)}), bf16[16,4,32,128]{3,2,1,0:T(8,128)(2,1)S(1)}, u32[]{:S(2)}, u32[]{:S(2)}) async-start(bf16[16,4,32,128]{3,2,1,0:T(8,128)(2,1)} %bitcast.4), calls=%async_computation | async-start | bytes 1048576 | tf_op jit(solution)/shard_map/all_to_all | solution.py:338
  10.2 6.2 %shard_map.68 = (bf16[16,2,4,32,128]{4,3,2,1,0:T(8,128)(2,1)}, bf16[16,256,256]{2,1,0:T(8,128)(2,1)}, bf16[16,128,256]{2,1,0:T(8,128)(2,1)}, bf16[16,128,256]{2,1,0:T(8,128)(2,1)}, f32[16,1,256]{2,1,0:T(1,128)}) custom-call(bf16[32,128,128]{2,1,0:T(8,128)(2,1)} %refs_0_.1, f32[1,128]{1,0:T(1,128)} %bitcast.12, bf16[256,128]{1,0:T(8,128)(2,1)} %bitcast.14, ...), custom_call_target="tpu_custom_call" | custom-call | flops 6000000000 | bytes 8388608 | tf_op jit(solution)/shard_map/pallas_call | solution.py:39
  16.4 5.3 %all-to-all-done.refs_1_ = bf16[16,4,32,128]{3,2,1,0:T(8,128)(2,1)S(1)} async-done(((bf16[16,4,32,128]{3,2,1,0:T(8,128)(2,1)}), bf16[16,4,32,128]{3,2,1,0:T(8,128)(2,1)S(1)}, u32[]{:S(2)}, u32[]{:S(2)}) %all-to-all-start) | async-done | bytes 524320 | tf_op jit(solution)/shard_map/all_to_all | solution.py:338
  21.7 1.9 %collective-permute-start.1 = (bf16[16,4,32,128]{3,2,1,0:T(8,128)(2,1)S(1)}, bf16[16,4,32,128]{3,2,1,0:T(8,128)(2,1)S(1)}, u32[]{:S(2)}, u32[]{:S(2)}) collective-permute-start(bf16[16,4,32,128]{3,2,1,0:T(8,128)(2,1)S(1)} %all-to-all-done.refs_1_), channel_id=1, source_target_pairs={{0,4},{4,0},{1,5},{5,1},{2,6},{6,2},{3,7},{7,3},{8,12},{12,8},{9,1... | collective-permute-start | bytes 1572872 | tf_op jit(solution)/shard_map/ppermute | solution.py:327
  23.7 3.7 %all-to-all-start.1 = ((bf16[16,2,4,32,128]{4,3,2,1,0:T(8,128)(2,1)}), bf16[16,2,4,32,128]{4,3,2,1,0:T(8,128)(2,1)S(1)}, u32[]{:S(2)}, u32[]{:S(2)}) async-start(bf16[16,2,4,32,128]{4,3,2,1,0:T(8,128)(2,1)} %get-tuple-element.17), calls=%async_computation.1 | async-start | bytes 2097152 | tf_op jit(solution)/shard_map/all_to_all | solution.py:342
  27.3 0.1 collective-permute-start
  27.4 6.8 %collective-permute-done.1.refs_3_ = bf16[16,4,32,128]{3,2,1,0:T(8,128)(2,1)S(1)} collective-permute-done((bf16[16,4,32,128]{3,2,1,0:T(8,128)(2,1)S(1)}, bf16[16,4,32,128]{3,2,1,0:T(8,128)(2,1)S(1)}, u32[]{:S(2)}, u32[]{:S(2)}) %collective-permute-start.1) | collective-permute-done | bytes 524320 | tf_op jit(solution)/shard_map/ppermute | solution.py:327
  34.2 0.0 collective-permute-start.2
  34.2 9.2 %all-to-all-done.1.refs_0_ = bf16[16,2,4,32,128]{4,3,2,1,0:T(8,128)(2,1)S(1)} async-done(((bf16[16,2,4,32,128]{4,3,2,1,0:T(8,128)(2,1)}), bf16[16,2,4,32,128]{4,3,2,1,0:T(8,128)(2,1)S(1)}, u32[]{:S(2)}, u32[]{:S(2)}) %all-to-all-start.1) | async-done | bytes 1048608 | tf_op jit(solution)/shard_map/all_to_all | solution.py:342
  43.4 0.0 collective-permute-done.2.refs_4_
  43.4 2.2 %shard_map.70 = bf16[16,2,4,32,128]{4,3,2,1,0:T(8,128)(2,1)S(1)} custom-call(bf16[16,2,4,32,128]{4,3,2,1,0:T(8,128)(2,1)S(1)} %all-to-all-done.1.refs_0_, bf16[16,4,32,128]{3,2,1,0:T(8,128)(2,1)S(1)} %all-to-all-done.refs_1_, bf16[16,4,32,128]{3,2,1,0:T(8,128)(2,1)S(1)} %collective-permute-done.refs_2_, ...), custom_call_target="tpu_custom_call" | custom-call | flops 4000000000 | bytes 5242880 | tf_op jit(solution)/shard_map/pallas_call | solution.py:39
  45.6 19.1 %all_to_all.25.refs_0_ = bf16[16,2,4,32,128]{4,3,2,1,0:T(8,128)(2,1)S(1)} all-to-all(bf16[16,2,4,32,128]{4,3,2,1,0:T(8,128)(2,1)S(1)} %shard_map.70), channel_id=1, replica_groups=mesh['ia'=16,'z_lo'=2,'core'=2,'col'=2] {'ia'}, dimensions={0} | all-to-all | bytes 2097152 | tf_op jit(solution)/shard_map/all_to_all | solution.py:346
  64.7 3.5 %shard_map.71 = (bf16[16,128,256]{2,1,0:T(8,128)(2,1)S(1)}, bf16[256,128]{1,0:T(8,128)(2,1)S(1)}) custom-call(bf16[16,2,4,32,128]{4,3,2,1,0:T(8,128)(2,1)S(1)} %all_to_all.25.refs_0_, bf16[16,256,256]{2,1,0:T(8,128)(2,1)} %get-tuple-element.19.refs_1_, bf16[16,128,256]{2,1,0:T(8,128)(2,1)} %get-tuple-element.20.refs_2_, bf16[256,128]{1,0:T(8,128)(2,1)} %bitcast.15), custom_call_target="tpu_custom_call" | custom-call | flops 6000000000 | bytes 8388608 | tf_op jit(solution)/shard_map/pallas_call | solution.py:39
  68.2 3.7 %collective-permute-start.3 = (bf16[16,128,256]{2,1,0:T(8,128)(2,1)S(1)}, bf16[16,128,256]{2,1,0:T(8,128)(2,1)S(1)}, u32[]{:S(2)}, u32[]{:S(2)}) collective-permute-start(bf16[16,128,256]{2,1,0:T(8,128)(2,1)S(1)} %get-tuple-element.25.own_ref), channel_id=1, source_target_pairs={{0,1},{1,0},{2,3},{3,2},{4,5},{5,4},{6,7},{7,6},{8,9},{9,8},{10,11... | collective-permute-start | bytes 3145736 | tf_op jit(solution)/shard_map/ppermute | solution.py:327
  71.8 10.6 %all_to_all.26.pieces_ref = bf16[32,8,128]{2,1,0:T(8,128)(2,1)S(1)} all-to-all(bf16[32,8,128]{2,1,0:T(8,128)(2,1)S(1)} %bitcast.10), channel_id=1, replica_groups=mesh['ia'=16,'z_lo'=2,'core'=2,'col'=2] {'ia','core'}, dimensions={0} | all-to-all | bytes 131072 | tf_op jit(solution)/shard_map/all_to_all | solution.py:351
  82.4 0.8 shard_map.72
  83.2 4.6 %all-to-all-start.4 = ((bf16[128,8,128]{2,1,0:T(8,128)(2,1)}), bf16[128,8,128]{2,1,0:T(8,128)(2,1)S(1)}, u32[]{:S(2)}, u32[]{:S(2)}) async-start(bf16[128,8,128]{2,1,0:T(8,128)(2,1)} %shard_map.72), calls=%async_computation.4 | async-start | bytes 524288 | tf_op jit(solution)/shard_map/all_to_all | solution.py:355
  87.7 1.3 %shard_map.73.unit_ref = bf16[16,128,256]{2,1,0:T(8,128)(2,1)S(1)} custom-call(bf16[16,128,256]{2,1,0:T(8,128)(2,1)} %get-tuple-element.23.x_ref), custom_call_target="tpu_custom_call" | custom-call | flops 1000000000 | bytes 1048576 | tf_op jit(solution)/shard_map/pallas_call | solution.py:39
  89.0 5.7 %collective-permute-done.3.other_ref = bf16[16,128,256]{2,1,0:T(8,128)(2,1)S(1)} collective-permute-done((bf16[16,128,256]{2,1,0:T(8,128)(2,1)S(1)}, bf16[16,128,256]{2,1,0:T(8,128)(2,1)S(1)}, u32[]{:S(2)}, u32[]{:S(2)}) %collective-permute-start.3) | collective-permute-done | bytes 1048608 | tf_op jit(solution)/shard_map/ppermute | solution.py:327
  94.7 3.4 %shard_map.74 = bf16[32,128,128]{2,1,0:T(8,128)(2,1)} custom-call(bf16[16,128,256]{2,1,0:T(8,128)(2,1)S(1)} %shard_map.73.unit_ref, f32[16,1,256]{2,1,0:T(1,128)} %get-tuple-element.24.inv_ref, f32[1,128]{1,0:T(1,128)} %bitcast.13, bf16[16,128,256]{2,1,0:T(8,128)(2,1)S(1)} %get-tuple-element.25.own_ref, ...), custom_call_target="tpu_custom_call" | custom-call | flops 1000000000 | bytes 4194304 | tf_op jit(solution)/shard_map/pallas_call | solution.py:39
  98.1 0.1 all-to-all-done.4.refs_0_
  98.2 0.8 shard_map.75
  (2 shorter events, 0.0 us)
Async XLA Ops:
  0.6 1.0 %copy-start = (bf16[32,64,128]{2,1,0:T(8,128)(2,1)S(1)}, bf16[32,64,128]{2,1,0:T(8,128)(2,1)}, u32[]{:S(2)}) copy-start(bf16[32,64,128]{2,1,0:T(8,128)(2,1)} %x_ref.1) | copy-start | bytes 1572868
  3.1 18.7 %all-to-all-start = ((bf16[16,4,32,128]{3,2,1,0:T(8,128)(2,1)}), bf16[16,4,32,128]{3,2,1,0:T(8,128)(2,1)S(1)}, u32[]{:S(2)}, u32[]{:S(2)}) async-start(bf16[16,4,32,128]{3,2,1,0:T(8,128)(2,1)} %bitcast.4), calls=%async_computation | async-start | bytes 1048576 | tf_op jit(solution)/shard_map/all_to_all | solution.py:338
  21.7 12.4 %collective-permute-start.1 = (bf16[16,4,32,128]{3,2,1,0:T(8,128)(2,1)S(1)}, bf16[16,4,32,128]{3,2,1,0:T(8,128)(2,1)S(1)}, u32[]{:S(2)}, u32[]{:S(2)}) collective-permute-start(bf16[16,4,32,128]{3,2,1,0:T(8,128)(2,1)S(1)} %all-to-all-done.refs_1_), channel_id=1, source_target_pairs={{0,4},{4,0},{1,5},{5,1},{2,6},{6,2},{3,7},{7,3},{8,12},{12,8},{9,1... | collective-permute-start | bytes 1572872 | tf_op jit(solution)/shard_map/ppermute | solution.py:327
  23.7 19.8 %all-to-all-start.1 = ((bf16[16,2,4,32,128]{4,3,2,1,0:T(8,128)(2,1)}), bf16[16,2,4,32,128]{4,3,2,1,0:T(8,128)(2,1)S(1)}, u32[]{:S(2)}, u32[]{:S(2)}) async-start(bf16[16,2,4,32,128]{4,3,2,1,0:T(8,128)(2,1)} %get-tuple-element.17), calls=%async_computation.1 | async-start | bytes 2097152 | tf_op jit(solution)/shard_map/all_to_all | solution.py:342
  27.3 6.9 %collective-permute-start = (bf16[16,4,32,128]{3,2,1,0:T(8,128)(2,1)S(1)}, bf16[16,4,32,128]{3,2,1,0:T(8,128)(2,1)S(1)}, u32[]{:S(2)}, u32[]{:S(2)}) collective-permute-start(bf16[16,4,32,128]{3,2,1,0:T(8,128)(2,1)S(1)} %all-to-all-done.refs_1_), channel_id=1, source_target_pairs={{0,2},{2,0},{1,3},{3,1},{4,6},{6,4},{5,7},{7,5},{8,10},{10,8},{9,1... | collective-permute-start | bytes 1572872 | tf_op jit(solution)/shard_map/ppermute | solution.py:327
  34.2 9.3 %collective-permute-start.2 = (bf16[16,4,32,128]{3,2,1,0:T(8,128)(2,1)S(1)}, bf16[16,4,32,128]{3,2,1,0:T(8,128)(2,1)S(1)}, u32[]{:S(2)}, u32[]{:S(2)}) collective-permute-start(bf16[16,4,32,128]{3,2,1,0:T(8,128)(2,1)S(1)} %collective-permute-done.1.refs_3_), channel_id=1, source_target_pairs={{0,2},{2,0},{1,3},{3,1},{4,6},{6,4},{5,7},{7,5},{8,10},{10,8},{9,1... | collective-permute-start | bytes 1572872 | tf_op jit(solution)/shard_map/ppermute | solution.py:327
  68.2 26.6 %collective-permute-start.3 = (bf16[16,128,256]{2,1,0:T(8,128)(2,1)S(1)}, bf16[16,128,256]{2,1,0:T(8,128)(2,1)S(1)}, u32[]{:S(2)}, u32[]{:S(2)}) collective-permute-start(bf16[16,128,256]{2,1,0:T(8,128)(2,1)S(1)} %get-tuple-element.25.own_ref), channel_id=1, source_target_pairs={{0,1},{1,0},{2,3},{3,2},{4,5},{5,4},{6,7},{7,6},{8,9},{9,8},{10,11... | collective-permute-start | bytes 3145736 | tf_op jit(solution)/shard_map/ppermute | solution.py:327
  83.2 15.1 %all-to-all-start.4 = ((bf16[128,8,128]{2,1,0:T(8,128)(2,1)}), bf16[128,8,128]{2,1,0:T(8,128)(2,1)S(1)}, u32[]{:S(2)}, u32[]{:S(2)}) async-start(bf16[128,8,128]{2,1,0:T(8,128)(2,1)} %shard_map.72), calls=%async_computation.4 | async-start | bytes 524288 | tf_op jit(solution)/shard_map/all_to_all | solution.py:355
